TPU v7x, 32 devices: a whole 2x2x4 slice. The times are simulated.
32 devices in a mesh: dp: 8 (over z, x), tensor: 4 (over y, core).
Axes of the slice: x: 2, y: 2, z: 4, core: 2. Of those that a mesh axis runs over, the one named last changes fastest.
Arguments:
- latents: bfloat16 [32, 512, 1024], P(('dp', 'tensor')), may hold values from -6 to 6
- cotangent: bfloat16 [32, 512, 1024], P(('dp', 'tensor')), may hold values from -6 to 6
- counts: int32 [16], replicated, may hold values from 1 to 3, as said below
- assign: int32 [16], replicated, may hold values from 0 to 7, as said below
- pre_gain: float32 [1024], replicated, may hold values from 0.1 to 1.9
- pre_shift: float32 [1024], replicated, may hold values from -1.75 to 1.75
- w_query: bfloat16 [1024, 1024], P(None, 'tensor'), may hold values from -0.375 to 0.375
- b_query: float32 [1024], P('tensor'), may hold values from -3 to 3
- w_key: bfloat16 [1024, 1024], P(None, 'tensor'), may hold values from -0.1875 to 0.1875
- w_value: bfloat16 [1024, 1024], P(None, 'tensor'), may hold values from -0.1875 to 0.1875
- b_value: float32 [1024], P('tensor'), may hold values from -1.75 to 1.75
- w_out: bfloat16 [1024, 1024], P('tensor'), may hold values from -0.75 to 0.75
- b_out: float32 [1024], replicated, may hold values from -1.75 to 1.75
- mid_gain: float32 [1024], replicated, may hold values from 0.1 to 1.9
- mid_shift: float32 [1024], replicated, may hold values from -1.75 to 1.75
- w_up: bfloat16 [1024, 1024], P(None, 'tensor'), may hold values from -0.1875 to 0.1875
- b_up: float32 [1024], P('tensor'), may hold values from -1.75 to 1.75
- w_down: bfloat16 [1024, 1024], P('tensor'), may hold values from -0.25 to 0.25
- b_down: float32 [1024], replicated, may hold values from -1.75 to 1.75
Outputs:
- latents_out: bfloat16 [32, 512, 1024], P(('dp', 'tensor'))
- latents_grad: float32 [32, 512, 1024], P(('dp', 'tensor'))
- pregain_grad: float32 [1024], replicated
- preshift_grad: float32 [1024], replicated
- wquery_grad: float32 [1024, 1024], P(None, 'tensor')
- bquery_grad: float32 [1024], P('tensor')
- wkey_grad: float32 [1024, 1024], P(None, 'tensor')
- wvalue_grad: float32 [1024, 1024], P(None, 'tensor')
- bvalue_grad: float32 [1024], P('tensor')
- wout_grad: float32 [1024, 1024], P('tensor')
- bout_grad: float32 [1024], replicated
- midgain_grad: float32 [1024], replicated
- midshift_grad: float32 [1024], replicated
- wup_grad: float32 [1024, 1024], P(None, 'tensor')
- bup_grad: float32 [1024], P('tensor')
- wdown_grad: float32 [1024, 1024], P('tensor')
- bdown_grad: float32 [1024], replicated
Inputs may be any that keep to these rules, and one draw needn't show every extreme that they name: The counts of the 2 images of one data index add up to at most 4, and to exactly 4 on at least one data index. `assign`: each data index holds exactly 2 images.
All inputs are finite; a program needn't handle non-finite values.
Results may differ from a plain program's by a relative error of at most 0.017.
Values may be sent and summed in bfloat16 or wider, within the bound.
A program may use at most 128 MiB of HBM per device.

v0:
```python
from functools import partial
import math

import jax
import jax.numpy as jnp
from jax import lax
from jax.sharding import PartitionSpec as P

HEAD = 128


epsilon = 1e-05


def normalize(inputs, norm_gain, norm_shift):
    center = jnp.mean(inputs, axis=-1, keepdims=True)
    centered = inputs - center
    inverse = lax.rsqrt(jnp.mean(centered * centered, axis=-1, keepdims=True) + epsilon)
    scaled = centered * inverse
    return (scaled * norm_gain + norm_shift, scaled, inverse)


def norm_backward(upstream, scaled, inverse, norm_gain):
    weighted = upstream * norm_gain
    first_mean = jnp.mean(weighted, axis=-1, keepdims=True)
    second_mean = jnp.mean(weighted * scaled, axis=-1, keepdims=True)
    return inverse * (weighted - first_mean - scaled * second_mean)


def split_heads(packed, attn_width):
    crop_count, length = (packed.shape[0], packed.shape[1])
    return [
        packed[:, :, member * attn_width : (member + 1) * attn_width].reshape(
            crop_count, length, attn_width // HEAD, HEAD
        )
        for member in range(3)
    ]


def attend_forward(queries, key_rows, values, scaling):
    scores = (
        jnp.einsum("cqhd,ckhd->chqk", queries, key_rows, preferred_element_type=jnp.float32)
        * scaling
    )
    row_max = jnp.max(scores, axis=-1, keepdims=True)
    exponent = jnp.exp(scores - row_max)
    summed = jnp.sum(exponent, axis=-1, keepdims=True)
    attn_probs = (exponent / summed).astype(jnp.bfloat16)
    logsum = row_max + jnp.log(summed)
    mixed = jnp.einsum("chqk,ckhd->cqhd", attn_probs, values, preferred_element_type=jnp.float32)
    return (mixed.astype(jnp.bfloat16), logsum)


def attend_backward(queries, key_rows, values, logsum, grad_mixed, scaling):
    scores = (
        jnp.einsum("cqhd,ckhd->chqk", queries, key_rows, preferred_element_type=jnp.float32)
        * scaling
    )
    attn_probs = jnp.exp(scores - logsum)
    grad_probs = jnp.einsum(
        "cqhd,ckhd->chqk", grad_mixed, values, preferred_element_type=jnp.float32
    )
    inner = jnp.sum(attn_probs * grad_probs, axis=-1, keepdims=True)
    grad_scores = (attn_probs * (grad_probs - inner)).astype(jnp.bfloat16)
    grad_queries = (
        jnp.einsum("chqk,ckhd->cqhd", grad_scores, key_rows, preferred_element_type=jnp.float32)
        * scaling
    ).astype(jnp.bfloat16)
    grad_keys = (
        jnp.einsum("chqk,cqhd->ckhd", grad_scores, queries, preferred_element_type=jnp.float32)
        * scaling
    ).astype(jnp.bfloat16)
    grad_values = jnp.einsum(
        "chqk,cqhd->ckhd",
        attn_probs.astype(jnp.bfloat16),
        grad_mixed,
        preferred_element_type=jnp.float32,
    ).astype(jnp.bfloat16)
    crop_count, length = (queries.shape[0], queries.shape[1])
    return jnp.concatenate(
        [
            member.reshape(crop_count, length, -1)
            for member in (grad_queries, grad_keys, grad_values)
        ],
        axis=-1,
    )


def shards(
    latents,
    cotangent,
    counts,
    assign,
    pre_gain,
    pre_shift,
    w_query,
    b_query,
    w_key,
    w_value,
    b_value,
    w_out,
    b_out,
    mid_gain,
    mid_shift,
    w_up,
    b_up,
    w_down,
    b_down,
):
    local_rows = latents.astype(jnp.float32)
    local_crops = latents.shape[0]
    group_total = jnp.sum(jnp.where(assign == lax.axis_index("dp"), counts, 0))
    slot_ids = lax.axis_index("tensor") * local_crops + jnp.arange(local_crops, dtype=jnp.int32)
    live_mask = (slot_ids < group_total).astype(jnp.float32)[:, None, None]
    scaling = 1.0 / math.sqrt(HEAD)
    attn_width = w_query.shape[1]
    w_joined = jnp.concatenate([w_query, w_key, w_value], axis=1)
    b_joined = jnp.concatenate([b_query, jnp.zeros_like(b_query), b_value])
    normed_pre, scaled_pre, inverse_pre = normalize(local_rows, pre_gain, pre_shift)
    normed_pre = normed_pre.astype(jnp.bfloat16)
    gathered_pre = lax.all_gather(normed_pre, "tensor", axis=0, tiled=True)
    joined = (
        jnp.dot(gathered_pre, w_joined, preferred_element_type=jnp.float32) + b_joined
    ).astype(jnp.bfloat16)
    queries, key_rows, values = split_heads(joined, attn_width)
    mixed, logsum = attend_forward(queries, key_rows, values, scaling)
    mixed_flat = mixed.reshape(mixed.shape[0], mixed.shape[1], attn_width)
    hidden = (
        local_rows
        + lax.psum_scatter(
            jnp.dot(mixed_flat, w_out, preferred_element_type=jnp.float32),
            "tensor",
            scatter_dimension=0,
            tiled=True,
        )
        + b_out
    )
    normed_mid, scaled_mid, inverse_mid = normalize(hidden, mid_gain, mid_shift)
    normed_mid = normed_mid.astype(jnp.bfloat16)
    gathered_mid = lax.all_gather(normed_mid, "tensor", axis=0, tiled=True)
    upward = jnp.dot(gathered_mid, w_up, preferred_element_type=jnp.float32) + b_up
    activated = jax.nn.gelu(upward, approximate=True).astype(jnp.bfloat16)
    result = (
        hidden
        + lax.psum_scatter(
            jnp.dot(activated, w_down, preferred_element_type=jnp.float32).astype(jnp.bfloat16),
            "tensor",
            scatter_dimension=0,
            tiled=True,
        ).astype(jnp.float32)
        + b_down
    )
    latents_out = (result * live_mask).astype(jnp.bfloat16)
    grad_result = cotangent * live_mask.astype(jnp.bfloat16)
    mlp_inputs, grad_rows = (
        lax.all_gather(normed_mid, "tensor", axis=0, tiled=True),
        lax.all_gather(grad_result, "tensor", axis=0, tiled=True),
    )
    up_again = jnp.dot(mlp_inputs, w_up, preferred_element_type=jnp.float32) + b_up
    act_again = jax.nn.gelu(up_again, approximate=True).astype(jnp.bfloat16)
    gd_wdown = jnp.einsum("cqf,cqd->fd", act_again, grad_rows, preferred_element_type=jnp.float32)
    grad_act = jnp.einsum("cqd,fd->cqf", grad_rows, w_down, preferred_element_type=jnp.float32)
    _, gelu_pull = jax.vjp(partial(jax.nn.gelu, approximate=True), up_again)
    grad_up = gelu_pull(grad_act)[0].astype(jnp.bfloat16)
    gd_wup = jnp.einsum("cqd,cqf->df", mlp_inputs, grad_up, preferred_element_type=jnp.float32)
    gd_bup = jnp.sum(grad_up, axis=(0, 1), dtype=jnp.float32)
    grad_mid = lax.psum_scatter(
        jnp.einsum("cqf,df->cqd", grad_up, w_up, preferred_element_type=jnp.float32),
        "tensor",
        scatter_dimension=0,
        tiled=True,
    )
    grad_hidden = grad_result.astype(jnp.float32) + norm_backward(
        grad_mid, scaled_mid, inverse_mid, mid_gain
    )
    middle_gain_gradient = jnp.sum(grad_mid * scaled_mid, axis=(0, 1))
    middle_shift_gradient = jnp.sum(grad_mid, axis=(0, 1))
    down_bias_gradient = jnp.sum(grad_result, axis=(0, 1), dtype=jnp.float32)
    grad_attn = grad_hidden.astype(jnp.bfloat16)
    output_bias_gradient = jnp.sum(grad_attn, axis=(0, 1), dtype=jnp.float32)
    attn_inputs, grad_attn_rows = (
        lax.all_gather(normed_pre, "tensor", axis=0, tiled=True),
        lax.all_gather(grad_attn, "tensor", axis=0, tiled=True),
    )
    joined_again = (
        jnp.dot(attn_inputs, w_joined, preferred_element_type=jnp.float32) + b_joined
    ).astype(jnp.bfloat16)
    queries_again, keys_again, values_again = split_heads(joined_again, attn_width)
    mixed_again, logsum_again = attend_forward(queries_again, keys_again, values_again, scaling)
    crop_count, length = (mixed_again.shape[0], mixed_again.shape[1])
    mixed_again_flat = mixed_again.reshape(crop_count, length, attn_width)
    gd_wout = jnp.einsum(
        "cqw,cqd->wd", mixed_again_flat, grad_attn_rows, preferred_element_type=jnp.float32
    )
    grad_mixed = jnp.einsum(
        "cqd,wd->cqw", grad_attn_rows, w_out, preferred_element_type=jnp.float32
    ).astype(jnp.bfloat16)
    grad_mixed = grad_mixed.reshape(crop_count, length, attn_width // HEAD, HEAD)
    grad_joined = attend_backward(
        queries_again, keys_again, values_again, logsum_again, grad_mixed, scaling
    )
    gd_wjoined = jnp.einsum(
        "cqd,cqk->dk", attn_inputs, grad_joined, preferred_element_type=jnp.float32
    )
    gd_bjoined = jnp.sum(grad_joined, axis=(0, 1), dtype=jnp.float32)
    prenorm_input_gradient = lax.psum_scatter(
        jnp.einsum("cqk,dk->cqd", grad_joined, w_joined, preferred_element_type=jnp.float32).astype(
            jnp.bfloat16
        ),
        "tensor",
        scatter_dimension=0,
        tiled=True,
    ).astype(jnp.float32)
    latents_grad = grad_hidden + norm_backward(
        prenorm_input_gradient, scaled_pre, inverse_pre, pre_gain
    )
    prenorm_gain_gradient = jnp.sum(prenorm_input_gradient * scaled_pre, axis=(0, 1))
    prenorm_shift_gradient = jnp.sum(prenorm_input_gradient, axis=(0, 1))
    (
        prenorm_gain_total,
        prenorm_shift_total,
        output_bias_total,
        middle_gain_total,
        middle_shift_total,
        down_bias_total,
    ) = lax.psum(
        (
            prenorm_gain_gradient,
            prenorm_shift_gradient,
            output_bias_gradient,
            middle_gain_gradient,
            middle_shift_gradient,
            down_bias_gradient,
        ),
        ("dp", "tensor"),
    )
    sum_wjoined, sum_bjoined, sum_wout, sum_wdown, sum_wup, sum_bup = lax.psum(
        (gd_wjoined, gd_bjoined, gd_wout, gd_wdown, gd_wup, gd_bup), "dp"
    )
    sum_wquery = sum_wjoined[:, :attn_width]
    sum_wkey = sum_wjoined[:, attn_width : 2 * attn_width]
    sum_wvalue = sum_wjoined[:, 2 * attn_width :]
    sum_bquery = sum_bjoined[:attn_width]
    sum_bvalue = sum_bjoined[2 * attn_width :]
    return (
        latents_out,
        latents_grad,
        prenorm_gain_total,
        prenorm_shift_total,
        sum_wquery,
        sum_bquery,
        sum_wkey,
        sum_wvalue,
        sum_bvalue,
        sum_wout,
        output_bias_total,
        middle_gain_total,
        middle_shift_total,
        sum_wup,
        sum_bup,
        sum_wdown,
        down_bias_total,
    )


def solution(mesh):
    return jax.shard_map(
        shards,
        mesh=mesh,
        in_specs=(
            P(("dp", "tensor"), None, None),
            P(("dp", "tensor"), None, None),
            P(),
            P(),
            P(),
            P(),
            P(None, "tensor"),
            P("tensor"),
            P(None, "tensor"),
            P(None, "tensor"),
            P("tensor"),
            P("tensor", None),
            P(),
            P(),
            P(),
            P(None, "tensor"),
            P("tensor"),
            P("tensor", None),
            P(),
        ),
        out_specs=(
            P(("dp", "tensor"), None, None),
            P(("dp", "tensor"), None, None),
            P(),
            P(),
            P(None, "tensor"),
            P("tensor"),
            P(None, "tensor"),
            P(None, "tensor"),
            P("tensor"),
            P("tensor", None),
            P(),
            P(),
            P(),
            P(None, "tensor"),
            P("tensor"),
            P("tensor", None),
            P(),
        ),
        check_vma=False,
    )
```

profile of v0, /device:TPU:0, one launch (start us, length us, event | category | flops | bytes accessed | tf_op | source)
XLA Modules:
  0.0 740.0 jit_solution(6482616116373510449)
XLA Ops:
  7.3 1.5 convert_reduce_fusion.2
  8.9 1.8 fusion.19
  10.7 1.4 fusion.15
  12.2 37.2 %all-gather.5.cloned.1.call-done = bf16[4,512,1024]{2,1,0:T(8,128)(2,1)} async-done(((bf16[1,512,1024]{2,1,0:T(8,128)(2,1)}), bf16[4,512,1024]{2,1,0:T(8,128)(2,1)}) %all-gather.5.cloned.1.call-update) | async-done | bytes 4194320 | tf_op jit(solution)/shard_map/all_gather | solution.py:121
  49.5 5.6 add_convert_fusion
  55.1 1.7 slice_bitcast_fusion
  56.8 0.5 copy.82
  57.4 1.9 copy.81
  59.3 1.3 multiply_reduce_fusion.1
  60.6 1.4 fusion
  62.1 1.8 copy-done.2
  63.9 2.0 fusion.30
  65.9 1.0 copy-done.15
  66.9 4.5 fusion.46
  71.5 71.5 %reduce-scatter.5.cloned.1.call-done = f32[1,512,1024]{2,1,0:T(8,128)} async-done(((f32[4,512,1024]{2,1,0:T(8,128)}), f32[1,512,1024]{2,1,0:T(8,128)}) %reduce-scatter.5.cloned.1.call-update) | async-done | bytes 2097168 | tf_op jit(solution)/shard_map/reduce_scatter | solution.py:130
  143.0 2.2 fusion.53
  145.2 0.3 multiply_reduce_fusion.4
  145.6 0.3 copy-done.21
  145.9 1.4 add_convert_fusion.1
  147.3 0.3 all-gather.9.cloned.1.call-start
  147.6 0.6 fusion.48
  148.9 2.5 convert_reduce_fusion.3
  151.5 30.4 %all-gather.7.cloned.1.call-done = bf16[4,512,1024]{2,1,0:T(8,128)(2,1)} async-done(((bf16[1,512,1024]{2,1,0:T(8,128)(2,1)}), bf16[4,512,1024]{2,1,0:T(8,128)(2,1)}) %all-gather.7.cloned.1.call-update) | async-done | bytes 4194320 | tf_op jit(solution)/shard_map/all_gather | solution.py:140
  181.9 4.9 fusion.43
  186.8 31.6 %all-gather.9.cloned.1.call-done = bf16[4,512,1024]{2,1,0:T(8,128)(2,1)} async-done(((bf16[1,512,1024]{2,1,0:T(8,128)(2,1)}), bf16[4,512,1024]{2,1,0:T(8,128)(2,1)}) %all-gather.9.cloned.1.call-update) | async-done | bytes 4194320 | tf_op jit(solution)/shard_map/all_gather | solution.py:157
  218.4 5.3 convert_reduce_fusion.4
  223.7 1.0 copy-done.14
  224.7 4.5 fusion.41
  229.2 0.0 reduce-scatter.7.cloned.1.call-start
  229.3 5.1 convolution_convert_fusion
  234.4 0.0 all-gather.11.cloned.1.call-start
  234.4 66.3 %reduce-scatter.9.cloned.1.call-done = f32[1,512,1024]{2,1,0:T(8,128)} async-done(((f32[4,512,1024]{2,1,0:T(8,128)}), f32[1,512,1024]{2,1,0:T(8,128)}) %reduce-scatter.9.cloned.1.call-update) | async-done | bytes 2097168 | tf_op jit(solution)/shard_map/reduce_scatter | solution.py:167
  300.8 2.5 multiply_reduce_fusion.2
  303.2 44.5 %reduce-scatter.7.cloned.1.call-done = bf16[1,512,1024]{2,1,0:T(8,128)(2,1)} async-done(((bf16[4,512,1024]{2,1,0:T(8,128)(2,1)}), bf16[1,512,1024]{2,1,0:T(8,128)(2,1)}) %reduce-scatter.7.cloned.1.call-update) | async-done | bytes 1048592 | tf_op jit(solution)/shard_map/reduce_scatter | solution.py:145
  347.8 4.1 convert_reduce_fusion.5
  352.0 4.9 convolution_bitcast_fusion.2
  357.0 2.6 convolution_bitcast_fusion.1
  359.5 27.0 %all-gather.11.cloned.1.call-done = bf16[4,512,1024]{2,1,0:T(8,128)(2,1)} async-done(((bf16[1,512,1024]{2,1,0:T(8,128)(2,1)}), bf16[4,512,1024]{2,1,0:T(8,128)(2,1)}) %all-gather.11.cloned.1.call-update) | async-done | bytes 4194320 | tf_op jit(solution)/shard_map/all_gather | solution.py:183
  386.6 3.6 convolution_convert_fusion.2
  390.2 5.2 fusion.31
  395.5 10.7 %multiply_reduce_fusion = (f32[4,2,512]{2,1,0:T(2,128)S(1)}, f32[4,2,512,512]{2,3,1,0:T(8,128)S(1)}) fusion(f32[4,2,512,512]{2,3,1,0:T(8,128)S(1)} %bitcast.77, f32[4,2,512]{2,1,0:T(2,128)S(1)} %bitcast.90, bf16[4,512,2,128]{1,3,2,0:T(8,128)(2,1)S(1)} %bitcast.84, bf16[4,64,2,8,128]{4,3,2,1,0:T(8,128)(2,1)S(1)} %copy-done.10), kind=kOutput, calls=%fused_computation.1 | convolution fusion | flops 545255424 | bytes 18907136 | tf_op jit(solution)/shard_map/cqhd,ckhd->chqk/dot_general | solution.py:60
  406.2 2.5 multiply_convert_fusion
  408.7 1.5 multiply_convert_fusion.1
  410.2 1.7 multiply_convert_fusion.2
  411.9 1.3 copy.68
  413.2 1.5 copy.66
  414.7 1.3 copy.67
  416.0 4.9 convolution_bitcast_fusion.3
  420.9 5.2 convolution_bitcast_fusion
  426.2 1.0 copy-done.34
  427.2 6.9 convolution_convert_fusion.1
  434.1 1.6 convert_reduce_fusion
  435.7 24.0 %all-reduce.1 = (f32[768]{0:T(1024)S(1)}, f32[256]{0:T(256)}) all-reduce(f32[768]{0:T(1024)S(1)} %convert_reduce_fusion, f32[256]{0:T(256)S(1)} %get-tuple-element.57), channel_id=1, replica_groups=mesh['dp'=8,'tensor'=4] {'dp'}, use_global_device_ids=true, to_apply=%region_22.23 | all-reduce | flops 1024 | bytes 8192 | tf_op jit(solution)/shard_map/psum | solution.py:237
  459.7 0.6 fusion.56
  460.3 177.1 %all-reduce.5.cloned.1.call-done = (f32[1024,768]{1,0:T(8,128)}, f32[256,1024]{1,0:T(8,128)}, f32[1024,256]{1,0:T(8,128)}, f32[256,1024]{1,0:T(8,128)}) async-done(((f32[1024,768]{1,0:T(8,128)}, f32[256,1024]{1,0:T(8,128)}, f32[1024,256]{1,0:T(8,128)}, f32[256,1024]{1,0:T(8,128)}), (f32[1024,768]{1,0:T(8,128)}, f32[256,1024]{1,0:T(8,128)}, f32[1024,256]{1,0:T(8,128)}, ...) | async-done | bytes 6291472 | tf_op jit(solution)/shard_map/psum | solution.py:237
  637.4 3.7 fusion.55
  641.1 42.5 %reduce-scatter.11.cloned.1.call-done = bf16[1,512,1024]{2,1,0:T(8,128)(2,1)} async-done(((bf16[4,512,1024]{2,1,0:T(8,128)(2,1)}), bf16[1,512,1024]{2,1,0:T(8,128)(2,1)}) %reduce-scatter.11.cloned.1.call-update) | async-done | bytes 1048592 | tf_op jit(solution)/shard_map/reduce_scatter | solution.py:206
  683.6 2.3 fusion.29
  685.9 40.0 %all-reduce = (f32[1024]{0:T(1024)}, f32[1024]{0:T(1024)}, f32[1024]{0:T(1024)}, f32[1024]{0:T(1024)}, f32[1024]{0:T(1024)}, /*index=5*/f32[1024]{0:T(1024)}) all-reduce(f32[1024]{0:T(1024)S(1)} %get-tuple-element.20, f32[1024]{0:T(1024)S(1)} %get-tuple-element.24, ...), channel_id=1, replica_groups=mesh['dp'=8,'tensor'=4] {'dp','tensor'}, use_global_device_ids=true, to_apply=%region_17.18 | all-reduce | flops 6144 | bytes 49152 | tf_op jit(solution)/shard_map/psum | solution.py:226
  725.9 3.7 fusion.18
  729.7 1.0 copy.98
  730.6 0.6 copy-done.17
  731.2 1.0 copy.99
  732.2 1.0 copy.100
  (102 shorter events, 0.7 us)
Async XLA Ops:
  7.2 211.2 %copy-start = (bf16[256,1024]{1,0:T(8,128)(2,1)S(1)}, bf16[256,1024]{1,0:T(8,128)(2,1)}, u32[]{:S(2)}) copy-start(bf16[256,1024]{1,0:T(8,128)(2,1)} %param.36) | copy-start | bytes 1572868
  7.2 3.4 copy-start.3
  7.2 3.4 copy-start.22
  7.2 3.4 copy-start.24
  7.2 42.2 %all-gather.5.cloned.1.call-start = ((), (), s32[]{:S(2)}) async-start(), calls=%async_computation.4 | async-start | bytes 5242880 | tf_op jit(solution)/shard_map/all_gather | solution.py:121
  8.8 3.4 copy-start.27
  8.8 3.4 copy-start.28
  8.9 40.6 %copy-start.33 = (bf16[1024,256]{1,0:T(8,128)(2,1)S(1)}, bf16[1024,256]{1,0:T(8,128)(2,1)}, u32[]{:S(2)}) copy-start(bf16[1024,256]{1,0:T(8,128)(2,1)} %param.28) | copy-start | bytes 1572868
  8.9 40.6 %copy-start.35 = (bf16[1024,256]{1,0:T(8,128)(2,1)S(1)}, bf16[1024,256]{1,0:T(8,128)(2,1)}, u32[]{:S(2)}) copy-start(bf16[1024,256]{1,0:T(8,128)(2,1)} %param.27) | copy-start | bytes 1572868
  8.9 40.6 %copy-start.36 = (bf16[1024,256]{1,0:T(8,128)(2,1)S(1)}, bf16[1024,256]{1,0:T(8,128)(2,1)}, u32[]{:S(2)}) copy-start(bf16[1024,256]{1,0:T(8,128)(2,1)} %param.25) | copy-start | bytes 1572868
  12.1 130.8 %reduce-scatter.5.cloned.1.call-start = ((), (), s32[]{:S(2)}) async-start(), calls=%async_computation.5 | async-start | bytes 10485760 | tf_op jit(solution)/shard_map/reduce_scatter | solution.py:130
  57.4 3.2 copy-start.7
  59.3 1.3 copy-start.5
  60.6 3.2 copy-start.2
  60.6 3.2 copy-start.9
  63.9 3.0 copy-start.19
  65.9 1.0 copy-start.15
  71.4 71.6 %copy-start.26 = (f32[1024]{0:T(1024)S(1)}, f32[1024]{0:T(1024)}, u32[]{:S(2)}) copy-start(f32[1024]{0:T(1024)} %param.31) | copy-start | bytes 12292
  71.4 110.5 %all-gather.7.cloned.1.call-start = ((), (), s32[]{:S(2)}) async-start(), calls=%async_computation.6 | async-start | bytes 5242880 | tf_op jit(solution)/shard_map/all_gather | solution.py:140
  145.2 0.7 copy-start.21
  145.2 0.7 copy-start.25
  145.9 1.7 copy-start.29
  145.9 1.7 copy-start.30
  147.3 71.1 %all-gather.9.cloned.1.call-start = ((), (), s32[]{:S(2)}) async-start(), calls=%async_computation.8 | async-start | bytes 5242880 | tf_op jit(solution)/shard_map/all_gather | solution.py:157
  151.4 67.0 %copy-start.37 = (f32[256]{0:T(256)S(1)}, f32[256]{0:T(256)}, u32[]{:S(2)}) copy-start(f32[256]{0:T(256)} %param.35) | copy-start | bytes 3076
  151.4 149.3 %reduce-scatter.9.cloned.1.call-start = ((), (), s32[]{:S(2)}) async-start(), calls=%async_computation.9 | async-start | bytes 10485760 | tf_op jit(solution)/shard_map/reduce_scatter | solution.py:167
  218.4 6.3 copy-start.20
  223.7 1.0 copy-start.14
  229.2 118.6 %reduce-scatter.7.cloned.1.call-start = ((), (), s32[]{:S(2)}) async-start(), calls=%async_computation.7 | async-start | bytes 5242880 | tf_op jit(solution)/shard_map/reduce_scatter | solution.py:145
  234.4 113.4 %copy-start.23 = (f32[1024]{0:T(1024)S(1)}, f32[1024]{0:T(1024)}, u32[]{:S(2)}) copy-start(f32[1024]{0:T(1024)} %param.37) | copy-start | bytes 12292
  234.4 152.2 %all-gather.11.cloned.1.call-start = ((), (), s32[]{:S(2)}) async-start(), calls=%async_computation.10 | async-start | bytes 5242880 | tf_op jit(solution)/shard_map/all_gather | solution.py:183
  351.9 285.5 %all-reduce.5.cloned.1.call-start = ((), (), s32[]{:S(2)}) async-start(), calls=%async_computation.12 | async-start | bytes 12582912 | tf_op jit(solution)/shard_map/psum | solution.py:237
  352.0 4.9 copy-start.32
  352.0 4.9 copy-start.38
  386.6 8.9 %slice-start = ((s8[8388608]{0:T(1024)(128)(4,1)}), s8[4194304]{0:T(1024)(128)(4,1)S(1)}, s32[]{:S(2)}) async-start(s8[8388608]{0:T(1024)(128)(4,1)} %bitcast.76), calls=%async_computation.13 | async-start | bytes 8388608
  390.2 5.3 slice-start.1
  390.2 5.3 copy-start.10
  406.2 2.5 copy-start.6
  408.7 1.5 copy-start.8
  416.0 4.9 copy-start.11
  416.0 4.9 copy-start.12
  416.0 4.9 copy-start.31
  426.1 1.0 copy-start.34
  426.2 257.4 %reduce-scatter.11.cloned.1.call-start = ((), (), s32[]{:S(2)}) async-start(), calls=%async_computation.11 | async-start | bytes 5242880 | tf_op jit(solution)/shard_map/reduce_scatter | solution.py:206
  637.4 46.2 %copy-start.4 = (bf16[1,512,1024]{2,1,0:T(8,128)(2,1)S(1)}, bf16[1,512,1024]{2,1,0:T(8,128)(2,1)}, u32[]{:S(2)}) copy-start(bf16[1,512,1024]{2,1,0:T(8,128)(2,1)} %param.19) | copy-start | bytes 3145732
  683.6 42.3 %copy-start.13 = (bf16[1,512,1024]{2,1,0:T(8,128)(2,1)S(1)}, bf16[1,512,1024]{2,1,0:T(8,128)(2,1)}, u32[]{:S(2)}) copy-start(bf16[1,512,1024]{2,1,0:T(8,128)(2,1)} %reduce-scatter.11.cloned.1.call-done) | copy-start | bytes 3145732
  725.9 3.7 copy-start.18
  729.6 1.6 copy-start.17
  729.6 2.6 copy-start.16
  729.7 3.5 copy-start.1
Sparse Core Ops, SparseCore 0:
  12.2 37.1 all-gather.4
  71.5 71.3 reduce-scatter.4
  147.4 34.4 all-gather.6
  183.9 34.4 all-gather.8
  229.4 71.3 reduce-scatter.8
  303.2 44.5 reduce-scatter.6
  352.1 34.4 all-gather.10
  426.3 211.0 all-reduce.4
  639.9 43.6 reduce-scatter.10
where the time goes:
time: 745 us; the launch traced here: 740 us
  waiting for transfers between devices  528 us (71%)
  matrix products  80.6 us (11%)
  blocking collectives  64 us (9%)
  other arithmetic  29.9 us (4%)
  local copies, waits for them, and re-layouts  21.2 us (3%)
  between operations  15.3 us (2%)
    psum x1, waiting for transfers between devices, shards(): lax.psum((gd_wjoined, gd_bjoined, gd_wout, gd_wdown, gd_wup, gd_bup), 'dp')  177 us
    reduce_scatter x1, waiting for transfers between devices, shards(): lax.psum_scatter(jnp.dot(mixed_flat, w_out, preferred_element_type=jnp.fl...  71.5 us
    reduce_scatter x1, waiting for transfers between devices, shards(): lax.psum_scatter(jnp.einsum('cqf,df->cqd', grad_up, w_up, preferred_eleme...  66.3 us
    reduce_scatter x1, waiting for transfers between devices, shards(): lax.psum_scatter(jnp.dot(activated, w_down, preferred_element_type=jnp.fl...  44.5 us
    reduce_scatter x1, waiting for transfers between devices, shards(): lax.psum_scatter(jnp.einsum('cqk,dk->cqd', grad_joined, w_joined, preferr...  42.5 us
    psum x1, blocking collectives, shards(): lax.psum((prenorm_gain_gradient, prenorm_shift_gradient, output_bias_grad...  40 us
    all_gather x1, waiting for transfers between devices, shards(): gathered_pre = lax.all_gather(normed_pre, 'tensor', axis=0, tiled=True)  37.2 us
    all_gather x1, waiting for transfers between devices, shards(): lax.all_gather(grad_result, 'tensor', axis=0, tiled=True)  31.6 us
  transfers between devices with their start and end apart: 9, of which 9 were waited for; matrix products, arithmetic and copies ran while one was open for 5% of the time, Pallas kernels for 0%

commit v1 on v0

v1 whole, which is shorter than its diff:
```python
from functools import partial
import math

import jax
import jax.numpy as jnp
from jax import lax
from jax.sharding import PartitionSpec as P

HEAD = 128


epsilon = 1e-05


def normalize(inputs, norm_gain, norm_shift):
    center = jnp.mean(inputs, axis=-1, keepdims=True)
    centered = inputs - center
    inverse = lax.rsqrt(jnp.mean(centered * centered, axis=-1, keepdims=True) + epsilon)
    scaled = centered * inverse
    return (scaled * norm_gain + norm_shift, scaled, inverse)


def norm_backward(upstream, scaled, inverse, norm_gain):
    weighted = upstream * norm_gain
    first_mean = jnp.mean(weighted, axis=-1, keepdims=True)
    second_mean = jnp.mean(weighted * scaled, axis=-1, keepdims=True)
    return inverse * (weighted - first_mean - scaled * second_mean)


def shards(
    latents,
    cotangent,
    counts,
    assign,
    pre_gain,
    pre_shift,
    w_query,
    b_query,
    w_key,
    w_value,
    b_value,
    w_out,
    b_out,
    mid_gain,
    mid_shift,
    w_up,
    b_up,
    w_down,
    b_down,
):
    f32, bf16 = jnp.float32, jnp.bfloat16
    crops, length, width = latents.shape
    tensor = lax.axis_size("tensor")
    heads = width // HEAD
    group_total = jnp.sum(jnp.where(assign == lax.axis_index("dp"), counts, 0))
    slot_ids = lax.axis_index("tensor") * crops + jnp.arange(crops, dtype=jnp.int32)
    live = jnp.repeat((slot_ids < group_total).astype(f32), length)[:, None]
    scaling = 1.0 / math.sqrt(HEAD)

    def dot(left, right, dims):
        return lax.dot_general(left, right, (dims, ((), ())), preferred_element_type=f32)

    columns = jnp.concatenate([w_query.T, w_key.T, w_value.T, w_out, w_up.T, w_down], axis=0)
    per = w_query.shape[1]
    gathered = lax.all_gather(columns, "tensor", axis=0, tiled=False).reshape(tensor, 6, per, width)
    wq, wk, wv, wo, wu, wd = [gathered[:, i].reshape(tensor * per, width) for i in range(6)]
    bias = lax.all_gather(jnp.stack([b_query, b_value, b_up]), "tensor", axis=1, tiled=True)

    rows = latents.astype(f32).reshape(crops * length, width)
    normed, scaled, inverse = normalize(rows, pre_gain, pre_shift)
    normed = normed.astype(bf16)
    q = (dot(normed, wq, ((1,), (1,))) + bias[0]).astype(bf16)
    k = dot(normed, wk, ((1,), (1,))).astype(bf16)
    v = (dot(normed, wv, ((1,), (1,))) + bias[1]).astype(bf16)
    split = lambda a: a.reshape(crops, length, heads, HEAD)
    q4, k4, v4 = split(q), split(k), split(v)
    ein = partial(jnp.einsum, preferred_element_type=f32)
    probs = jax.nn.softmax(ein("cqhd,ckhd->chqk", q4, k4) * scaling, axis=-1)
    low = probs.astype(bf16)
    mixed = ein("chqk,ckhd->cqhd", low, v4).astype(bf16).reshape(crops * length, width)
    hidden = rows + (dot(mixed, wo, ((1,), (0,))) + b_out)
    normed2, scaled2, inverse2 = normalize(hidden, mid_gain, mid_shift)
    normed2 = normed2.astype(bf16)
    upward = dot(normed2, wu, ((1,), (1,))) + bias[2]
    act32, gelu_pull = jax.vjp(partial(jax.nn.gelu, approximate=True), upward)
    act = act32.astype(bf16)
    result = hidden + (dot(act, wd, ((1,), (0,))) + b_down)
    latents_out = (result * live).astype(bf16).reshape(latents.shape)
    gy = cotangent.reshape(crops * length, width) * live.astype(bf16)
    g_wd = dot(act, gy, ((0,), (0,)))
    gu = gelu_pull(dot(gy, wd, ((1,), (1,))))[0].astype(bf16)
    g_wu = dot(gu, normed2, ((0,), (0,)))
    gn2 = dot(gu, wu, ((1,), (0,)))
    gh = gy.astype(f32) + norm_backward(gn2, scaled2, inverse2, mid_gain)
    ga = gh.astype(bf16)
    g_wo = dot(mixed, ga, ((0,), (0,)))
    go = split(dot(ga, wo, ((1,), (1,))).astype(bf16))
    gp = ein("cqhd,ckhd->chqk", go, v4)
    gs = (probs * (gp - jnp.sum(probs * gp, axis=-1, keepdims=True))).astype(bf16)
    flat = lambda a: a.astype(bf16).reshape(crops * length, width)
    gq = flat(ein("chqk,ckhd->cqhd", gs, k4) * scaling)
    gk = flat(ein("chqk,cqhd->ckhd", gs, q4) * scaling)
    gv = flat(ein("chqk,cqhd->ckhd", low, go))
    g_wq, g_wk, g_wv = [dot(a, normed, ((0,), (0,))) for a in (gq, gk, gv)]
    gn1 = dot(gq, wq, ((1,), (0,))) + dot(gk, wk, ((1,), (0,))) + dot(gv, wv, ((1,), (0,)))
    latents_grad = (gh + norm_backward(gn1, scaled, inverse, pre_gain)).reshape(latents.shape)

    def total(parts):
        stacked = jnp.stack([p.astype(bf16).reshape(tensor, per, width) for p in parts], axis=1)
        part = lax.psum_scatter(stacked, "tensor", scatter_dimension=0, tiled=True)
        return lax.psum(part, "dp")[0].astype(f32)

    s_wd, s_wu, s_wo = total((g_wd, g_wu, g_wo))
    s_wq, s_wk, s_wv = total((g_wq, g_wk, g_wv))
    col = lambda a: jnp.sum(a, axis=0, dtype=f32)
    sums = lax.psum(
        jnp.stack(
            [
                col(gn1 * scaled),
                col(gn1),
                col(ga),
                col(gn2 * scaled2),
                col(gn2),
                col(gy),
                col(gq),
                col(gv),
                col(gu),
            ]
        ),
        ("dp", "tensor"),
    )
    mine = lax.dynamic_slice_in_dim(sums[6:], lax.axis_index("tensor") * per, per, axis=1)
    return (
        latents_out,
        latents_grad,
        sums[0],
        sums[1],
        s_wq.T,
        mine[0],
        s_wk.T,
        s_wv.T,
        mine[1],
        s_wo,
        sums[2],
        sums[3],
        sums[4],
        s_wu.T,
        mine[2],
        s_wd,
        sums[5],
    )


def solution(mesh):
    return jax.shard_map(
        shards,
        mesh=mesh,
        in_specs=(
            P(("dp", "tensor"), None, None),
            P(("dp", "tensor"), None, None),
            P(),
            P(),
            P(),
            P(),
            P(None, "tensor"),
            P("tensor"),
            P(None, "tensor"),
            P(None, "tensor"),
            P("tensor"),
            P("tensor", None),
            P(),
            P(),
            P(),
            P(None, "tensor"),
            P("tensor"),
            P("tensor", None),
            P(),
        ),
        out_specs=(
            P(("dp", "tensor"), None, None),
            P(("dp", "tensor"), None, None),
            P(),
            P(),
            P(None, "tensor"),
            P("tensor"),
            P(None, "tensor"),
            P(None, "tensor"),
            P("tensor"),
            P("tensor", None),
            P(),
            P(),
            P(),
            P(None, "tensor"),
            P("tensor"),
            P("tensor", None),
            P(),
        ),
        check_vma=False,
    )
```

time: 745 us -> 426 us (0.57)
  waiting for transfers between devices: 528 us -> 213 us
  local copies, waits for them, and re-layouts: 21.2 us -> 45.9 us
  blocking collectives: 64 us -> 49.2 us
  matrix products: 80.6 us -> 72 us
    reduce_scatter x4 -> x2, waiting for transfers between devices: 225 us -> 62.8 us  [total(): part = lax.psum_scatter(stacked, 'tensor', scatter_dimension=0, tiled=True)]
    psum x1, waiting for transfers between devices: 177 us -> 73.5 us  [total(): return lax.psum(part, 'dp')[0].astype(f32)]
    all_gather x4 -> x1, waiting for transfers between devices: 126 us -> 76.6 us  [shards(): lax.all_gather(columns, 'tensor', axis=0, tiled=False)]
    psum x2 -> x1, blocking collectives: 64 us -> 42.9 us  [shards(): lax.psum(jnp.stack([col(gn1 * scaled), col(gn1), col(ga), col(gn2 * scale...]
    another operation x0 -> x7, local copies, waits for them, and re-layouts: none -> 16.7 us  [the longest x3 11.8 us: total(): jnp.stack([p.astype(bf16).reshape(tensor, per, width) for p in parts], ax...]
    dot_general x18 -> x23, matrix products: 80.6 us -> 66.8 us  [the longest x18 44 us: dot(): lax.dot_general(left, right, (dims, ((), ())), preferred_element_type=f32)]
    reduce_sum x6 -> x1, other arithmetic: 14.4 us -> 0.93 us  [shards(): col = lambda a: jnp.sum(a, axis=0, dtype=f32)]
    another operation x0 -> x3, other arithmetic: none -> 9.87 us  [the longest x2 9.86 us: total(): jnp.stack([p.astype(bf16).reshape(tensor, per, width) for p in parts], ax...]
  transfers between devices with their start and end apart: 9 -> 4, of which waited for: 9 -> 4; matrix products, arithmetic and copies ran while one was open for 5% -> 18% of each run, Pallas kernels for 0% -> 0%
where the time goes in v1:
time: 426 us; the launch traced here: 419 us
  waiting for transfers between devices  213 us (50%)
  matrix products  72 us (17%)
  blocking collectives  49.2 us (12%)
  local copies, waits for them, and re-layouts  45.9 us (11%)
  other arithmetic  23.4 us (5%)
  between operations  15.5 us (4%)
    all_gather x1, waiting for transfers between devices, shards(): lax.all_gather(columns, 'tensor', axis=0, tiled=False)  76.6 us
    psum x1, waiting for transfers between devices, total(): return lax.psum(part, 'dp')[0].astype(f32)  73.5 us
    reduce_scatter x2, waiting for transfers between devices, total(): part = lax.psum_scatter(stacked, 'tensor', scatter_dimension=0, tiled=True)  62.8 us
    dot_general x18, matrix products, dot(): lax.dot_general(left, right, (dims, ((), ())), preferred_element_type=f32)  44 us
    psum x1, blocking collectives, shards(): lax.psum(jnp.stack([col(gn1 * scaled), col(gn1), col(ga), col(gn2 * scale...  42.9 us
    unnamed x84, local copies, waits for them, and re-layouts  14.1 us
    another operation x3, local copies, waits for them, and re-layouts, total(): jnp.stack([p.astype(bf16).reshape(tensor, per, width) for p in parts], ax...  11.8 us
    another operation x2, other arithmetic, total(): jnp.stack([p.astype(bf16).reshape(tensor, per, width) for p in parts], ax...  9.86 us
  transfers between devices with their start and end apart: 4, of which 4 were waited for; matrix products, arithmetic and copies ran while one was open for 18% of the time, Pallas kernels for 0%

profile of v1, /device:TPU:0, one launch (start us, length us, event | category | flops | bytes accessed | tf_op | source)
XLA Modules:
  0.0 419.4 jit_solution(4079117353360037108)
XLA Ops:
  7.3 1.3 copy.36
  8.6 1.2 copy.37
  10.3 0.9 bitcast_dynamic-update-slice_fusion.3
  11.2 0.9 bitcast_dynamic-update-slice_fusion.2
  12.0 0.8 bitcast_dynamic-update-slice_fusion.1
  12.9 0.8 constant_dynamic-update-slice_fusion.1
  13.7 0.8 bitcast_dynamic-update-slice_fusion
  14.6 0.8 constant_dynamic-update-slice_fusion
  15.5 0.6 fusion.59
  16.9 6.3 %all_gather.11 = f32[3,1024]{1,0:T(4,128)S(1)} all-gather(f32[3,256]{1,0:T(4,128)S(1)} %pad_maximum_fusion.2), channel_id=1, replica_groups=mesh['dp'=8,'tensor'=4] {'tensor'}, dimensions={1}, use_global_device_ids=true | all-gather | bytes 15360 | tf_op jit(solution)/shard_map/all_gather | solution.py:67
  23.4 0.4 fusion.18
  23.8 76.6 %all-gather.3.cloned.1.call-done = bf16[6144,1024]{1,0:T(8,128)(2,1)} async-done(((bf16[1536,1024]{1,0:T(8,128)(2,1)}), bf16[6144,1024]{1,0:T(8,128)(2,1)}) %all-gather.3.cloned.1.call-update) | async-done | bytes 12582928 | tf_op jit(solution)/shard_map/all_gather | solution.py:65
  100.4 9.0 %fusion.70 = (bf16[4,1,256,1024]{3,2,1,0:T(8,128)(2,1)}, bf16[4,1,256,1024]{3,2,1,0:T(8,128)(2,1)}, bf16[4,1,256,1024]{3,2,1,0:T(8,128)(2,1)}, bf16[4,1,256,1024...) fusion(bf16[4,6,256,1024]{3,2,1,0:T(8,128)(2,1)} %bitcast.191), kind=kLoop, calls=%fused_computation.118 | loop fusion | bytes 25165824 | tf_op jit(solution)/shard_map/slice | solution.py:66
  109.4 2.3 add_convert_fusion.1
  111.7 2.3 copy.63
  114.0 2.9 convolution_convert_fusion.7
  116.9 0.5 copy.64
  117.5 4.3 %fusion.40 = bf16[64,8,8,128]{3,2,1,0:T(8,128)(2,1)} fusion(bf16[1024,1024]{1,0:T(8,128)(2,1)} %bitcast.208, f32[1024]{0:T(1024)S(1)} %bitcast.240, bf16[1,512,1024]{2,1,0:T(8,128)(2,1)S(1)} %copy-done.1, f32[1024]{0:T(1024)S(1)} %copy-done.31, f32[1024]{0:T(1024)S(1)} %copy-done.24, f32[512]{0:T(512)S(1)} %add_rsqrt_fusion.1, ...), kind=kOutput, calls=%fused_computation.74 | convolution fusion | flops 1077936128 | bytes 4210688 | tf_op jit(solution)/shard_map/dot_general | solution.py:61
  121.8 5.2 %fusion.74 = (f32[8,512]{1,0:T(8,128)S(1)}, f32[8,512,512]{1,2,0:T(8,128)}) fusion(bf16[512,8,128]{0,2,1:T(8,128)(2,1)S(1)} %bitcast.203, bf16[512,8,128]{0,2,1:T(8,128)(2,1)S(1)} %bitcast.204), kind=kOutput, calls=%fused_computation.122 | convolution fusion | flops 543162880 | bytes 10502144 | tf_op jit(solution)/shard_map/sub | solution.py:78
  127.0 4.7 %fusion.34 = bf16[8,128,512]{2,1,0:T(8,128)(2,1)S(1)} fusion(bf16[64,8,8,128]{3,2,1,0:T(8,128)(2,1)} %fusion.40, f32[8,512,512]{1,2,0:T(8,128)} %get-tuple-element.72, f32[8,512]{1,0:T(8,128)S(1)} %get-tuple-element.71), kind=kOutput, calls=%fused_computation.70 | convolution fusion | flops 541589504 | bytes 10502144 | tf_op jit(solution)/shard_map/chqk,ckhd->cqhd/dot_general | solution.py:80
  131.8 1.4 fusion.75
  133.2 0.3 multiply_reduce_fusion.4
  133.5 1.2 copy-done.15
  134.7 1.3 fusion.63
  136.1 1.7 convolution_convert_fusion.2
  137.8 0.6 copy-done.12
  138.4 2.5 convert_reduce_fusion.2
  140.9 1.8 multiply_reduce_fusion.2
  142.7 1.5 convolution_convert_fusion.1
  144.3 0.9 convert_reduce_fusion.5
  145.2 1.3 convolution_convert_fusion
  146.5 3.4 pad_maximum_fusion.1
  150.0 4.5 %convolution_convert_fusion.6 = bf16[512,1024]{1,0:T(8,128)(2,1)} fusion(bf16[1024,1024]{1,0:T(8,128)(2,1)} %bitcast.196, f32[512,1024]{1,0:T(8,128)} %copy-done.5), kind=kOutput, calls=%fused_computation.72 | convolution fusion | flops 1074790400 | bytes 5242880 | tf_op jit(solution)/shard_map/dot_general | solution.py:61
  154.5 2.5 copy.65
  156.9 7.1 %convert_reduce_fusion.3 = (f32[8,128]{1,0:T(8,128)S(1)}, bf16[8,128,512]{2,1,0:T(8,128)(2,1)S(1)}) fusion(bf16[512,8,128]{0,2,1:T(8,128)(2,1)} %bitcast.218, f32[8,512,512]{1,2,0:T(8,128)} %get-tuple-element.72, f32[8,512]{1,0:T(8,128)S(1)} %get-tuple-element.71), kind=kOutput, calls=%fused_computation.43 | convolution fusion | flops 542637056 | bytes 10506240 | tf_op jit(solution)/shard_map/chqk,cqhd->ckhd/dot_general | solution.py:103
  164.0 2.7 convolution_convert_fusion.3
  166.7 3.9 copy.54
  170.7 6.2 %multiply_reduce_fusion = (f32[8,512]{1,0:T(8,128)S(1)}, f32[8,512,512]{1,2,0:T(8,128)S(1)}) fusion(f32[8,512,512]{1,2,0:T(8,128)} %get-tuple-element.72, f32[8,512]{1,0:T(8,128)S(1)} %get-tuple-element.71, bf16[512,8,128]{0,2,1:T(8,128)(2,1)} %bitcast.219, bf16[64,8,8,128]{3,2,1,0:T(8,128)(2,1)} %fusion.40), kind=kOutput, calls=%fused_computation.2 | convolution fusion | flops 543158272 | bytes 18907136 | tf_op jit(solution)/shard_map/cqhd,ckhd->chqk/dot_general | solution.py:98
  176.9 4.5 %multiply_convert_fusion = bf16[8,512,512]{1,2,0:T(8,128)(2,1)S(1)} fusion(f32[8,512,512]{1,2,0:T(8,128)S(1)} %get-tuple-element.77, f32[8,512]{1,0:T(8,128)S(1)} %get-tuple-element.76, f32[8,512,512]{1,2,0:T(8,128)} %get-tuple-element.72, f32[8,512]{1,0:T(8,128)S(1)} %get-tuple-element.71), kind=kLoop, calls=%fused_computation.1 | loop fusion | flops 8388608 | bytes 21004288 | tf_op jit(solution)/shard_map/convert_element_type | solution.py:99
  181.4 0.8 convert_reduce_fusion.4
  182.2 1.1 copy-done
  183.3 2.7 convolution_convert_fusion.5
  186.0 4.0 copy.52
  190.0 4.0 multiply_convert_fusion.1
  194.1 2.8 convolution_convert_fusion.4
  196.8 4.0 copy.53
  200.8 6.5 %pad_maximum_fusion = bf16[4,3,256,1024]{2,3,1,0:T(8,128)(2,1)} fusion(bf16[4,1,256,1024]{2,3,1,0:T(8,128)(2,1)} %copy.54, bf16[4,1,256,1024]{2,3,1,0:T(8,128)(2,1)} %copy.53, bf16[4,1,256,1024]{2,3,1,0:T(8,128)(2,1)} %copy.52), kind=kLoop, calls=%fused_computation.6 | loop fusion | flops 6291456 | bytes 12582912 | tf_op jit(solution)/shard_map/stack | solution.py:109
  207.6 1.4 reduce-scatter.5.cloned.1.call-done
  208.9 61.4 %reduce-scatter.3.cloned.1.call-done = bf16[1,3,256,1024]{2,3,1,0:T(8,128)(2,1)} async-done(((bf16[4,3,256,1024]{2,3,1,0:T(8,128)(2,1)}), bf16[1,3,256,1024]{2,3,1,0:T(8,128)(2,1)}) %reduce-scatter.3.cloned.1.call-update) | async-done | bytes 1572880 | tf_op jit(solution)/shard_map/reduce_scatter | solution.py:110
  270.4 3.3 fusion.77
  273.8 1.3 fusion.76
  275.6 3.3 fusion.17
  279.0 42.9 %psum.21 = f32[9,1024]{1,0:T(8,128)S(1)} all-reduce(f32[9,1024]{1,0:T(8,128)S(1)} %stack.61), channel_id=1, replica_groups=mesh['dp'=8,'tensor'=4] {'dp','tensor'}, use_global_device_ids=true, to_apply=%region_21.22 | all-reduce | flops 9216 | bytes 73728 | tf_op jit(solution)/shard_map/psum | solution.py:116
  321.9 0.7 fusion.72
  322.6 0.6 fusion.71
  323.2 4.4 %fusion.16 = f32[1,512,1024]{2,1,0:T(8,128)} fusion(f32[512,1024]{1,0:T(8,128)} %copy-done.5, bf16[1,512,1024]{2,1,0:T(8,128)(2,1)S(1)} %copy-done.1, f32[512,1024]{1,0:T(8,128)} %get-tuple-element.78, f32[512]{0:T(512)S(1)} %broadcast_multiply_fusion, f32[512]{0:T(512)S(1)} %broadcast_multiply_fusion.1, f32[1024]{0:T(1024)S(1)} %copy-done.24, ...), kind=kLoop, calls=%fused_computation.28 | loop fusion | flops 4718592 | bytes 7352320 | tf_op jit(solution)/shard_map/reshape | solution.py:106
  327.6 2.6 fusion.41
  330.2 73.5 %all-reduce.3.cloned.1.call-done = (bf16[1,3,256,1024]{2,3,1,0:T(8,128)(2,1)}, bf16[1,3,256,1024]{3,2,1,0:T(8,128)(2,1)}) async-done(((bf16[1,3,256,1024]{2,3,1,0:T(8,128)(2,1)}, bf16[1,3,256,1024]{3,2,1,0:T(8,128)(2,1)}), (bf16[1,3,256,1024]{2,3,1,0:T(8,128)(2,1)}, bf16[1,3,256,1024]{3,2,1,0:T(8,128)(2,1)})) %all-reduce.3.cloned.1.call-update) | async-done | bytes 3145744 | tf_op jit(solution)/shard_map/psum | solution.py:111
  403.7 1.7 convert_element_type.173
  405.4 1.7 slice_bitcast_fusion.3
  407.1 0.6 copy-done.16
  407.7 0.4 convert_element_type.177
  408.1 1.8 slice_bitcast_fusion
  409.9 2.5 copy.58
  (92 shorter events, 2.0 us)
Async XLA Ops:
  7.2 2.7 copy-start.18
  7.2 2.9 copy-start.19
  7.2 93.2 %all-gather.3.cloned.1.call-start = ((), (), s32[]{:S(2)}) async-start(), calls=%async_computation.4 | async-start | bytes 15728640 | tf_op jit(solution)/shard_map/all_gather | solution.py:65
  10.1 2.8 copy-start.20
  11.2 3.4 copy-start.21
  14.5 1.0 copy-start.28
  14.5 1.0 copy-start.29
  14.5 2.3 copy-start.25
  14.5 2.3 copy-start.26
  14.6 2.3 copy-start.27
  14.6 8.6 %copy-start.1 = (bf16[1,512,1024]{2,1,0:T(8,128)(2,1)S(1)}, bf16[1,512,1024]{2,1,0:T(8,128)(2,1)}, u32[]{:S(2)}) copy-start(bf16[1,512,1024]{2,1,0:T(8,128)(2,1)} %param.19) | copy-start | bytes 3145732
  15.5 193.5 %reduce-scatter.5.cloned.1.call-start = ((), (), s32[]{:S(2)}) async-start(), calls=%async_computation.3 | async-start | bytes 7864320 | tf_op jit(solution)/shard_map/reduce_scatter | solution.py:110
  100.4 9.0 %copy-start.24 = (f32[1024]{0:T(1024)S(1)}, f32[1024]{0:T(1024)}, u32[]{:S(2)}) copy-start(f32[1024]{0:T(1024)} %param.23) | copy-start | bytes 12292
  100.4 9.0 %copy-start.31 = (f32[1024]{0:T(1024)S(1)}, f32[1024]{0:T(1024)}, u32[]{:S(2)}) copy-start(f32[1024]{0:T(1024)} %param.24) | copy-start | bytes 12292
  109.4 2.3 copy-start.2
  117.5 4.3 %copy-start.10 = (bf16[512,1024]{0,1:T(8,128)(2,1)}, bf16[512,1024]{0,1:T(8,128)(2,1)S(1)}, u32[]{:S(2)}) copy-start(bf16[512,1024]{0,1:T(8,128)(2,1)S(1)} %copy.64) | copy-start | bytes 3145732
  117.5 4.3 %copy-start.9 = (bf16[512,1024]{0,1:T(8,128)(2,1)S(1)}, bf16[512,1024]{0,1:T(8,128)(2,1)}, u32[]{:S(2)}) copy-start(bf16[512,1024]{0,1:T(8,128)(2,1)} %copy.63) | copy-start | bytes 3145732
  127.0 4.8 %copy-start.4 = (bf16[4,1,256,1024]{3,2,1,0:T(8,128)(2,1)S(1)}, bf16[4,1,256,1024]{3,2,1,0:T(8,128)(2,1)}, u32[]{:S(2)}) copy-start(bf16[4,1,256,1024]{3,2,1,0:T(8,128)(2,1)} %get-tuple-element.48) | copy-start | bytes 6291460
  127.0 4.8 %copy-start.22 = (f32[1024]{0:T(1024)S(1)}, f32[1024]{0:T(1024)}, u32[]{:S(2)}) copy-start(f32[1024]{0:T(1024)} %param.31) | copy-start | bytes 12292
  133.1 1.6 copy-start.15
  133.1 1.6 copy-start.23
  133.1 1.6 copy-start.30
  134.7 1.4 copy-start.17
  136.1 1.7 copy-start.35
  136.1 2.3 copy-start.12
  145.2 1.3 copy-start.5
  149.9 120.4 %reduce-scatter.3.cloned.1.call-start = ((), (), s32[]{:S(2)}) async-start(), calls=%async_computation.2 | async-start | bytes 7864320 | tf_op jit(solution)/shard_map/reduce_scatter | solution.py:110
  164.0 2.7 copy-start.33
  176.9 4.5 %copy-start.11 = (bf16[512,1024]{0,1:T(8,128)(2,1)S(1)}, bf16[512,1024]{0,1:T(8,128)(2,1)}, u32[]{:S(2)}) copy-start(bf16[512,1024]{0,1:T(8,128)(2,1)} %copy-done.10) | copy-start | bytes 3145732
  181.4 1.9 copy-start
  183.3 2.7 copy-start.6
  194.0 2.8 copy-start.8
  207.3 196.4 %all-reduce.3.cloned.1.call-start = ((), (), s32[]{:S(2)}) async-start(), calls=%async_computation.5 | async-start | bytes 6291456 | tf_op jit(solution)/shard_map/psum | solution.py:111
  270.4 3.4 copy-start.3
  270.4 3.4 copy-start.7
  273.7 1.6 copy-start.14
  273.7 1.8 copy-start.34
  323.2 4.4 %copy-start.13 = (bf16[4,1,256,1024]{3,2,1,0:T(8,128)(2,1)S(1)}, bf16[4,1,256,1024]{3,2,1,0:T(8,128)(2,1)}, u32[]{:S(2)}) copy-start(bf16[4,1,256,1024]{3,2,1,0:T(8,128)(2,1)} %get-tuple-element.47) | copy-start | bytes 6291460
  323.2 4.4 %copy-start.32 = (f32[1024]{0:T(1024)S(1)}, f32[1024]{0:T(1024)}, u32[]{:S(2)}) copy-start(f32[1024]{0:T(1024)} %param.37) | copy-start | bytes 12292
  323.2 4.4 %copy-start.36 = (f32[512,1024]{1,0:T(8,128)S(1)}, f32[512,1024]{1,0:T(8,128)}, u32[]{:S(2)}) copy-start(f32[512,1024]{1,0:T(8,128)} %copy-done.35) | copy-start | bytes 6291460
  405.4 2.4 copy-start.16
Sparse Core Ops, SparseCore 0:
  15.6 84.7 all-gather.2
  150.0 58.8 reduce-scatter.4
  211.5 58.8 reduce-scatter.2
  273.8 129.7 all-reduce.2

commit v2 on v1

v2 whole, which is shorter than its diff:
```python
from functools import partial
import math

import jax
import jax.numpy as jnp
from jax import lax
from jax.experimental import pallas as pl
from jax.experimental.pallas import tpu as pltpu
from jax.sharding import PartitionSpec as P

HEAD = 128
EPS = 1e-05
CHUNKS = 12
BLOCK = 128
ROWS = 128
F32 = jnp.float32
BF16 = jnp.bfloat16
MESH = pl.DeviceIdType.MESH


def dot(left, right):
    return lax.dot_general(left, right, (((1,), (0,)), ((), ())), preferred_element_type=F32)


def dot_nt(left, right):
    return lax.dot_general(left, right, (((1,), (1,)), ((), ())), preferred_element_type=F32)


def dot_tn(left, right):
    return lax.dot_general(left, right, (((0,), (0,)), ((), ())), preferred_element_type=F32)


def aligned(start, size):
    return pl.ds(pl.multiple_of(start, size), size)


def row_stats(values):
    center = jnp.mean(values, axis=-1, keepdims=True)
    centered = values - center
    inverse = lax.rsqrt(jnp.mean(centered * centered, axis=-1, keepdims=True) + EPS)
    return centered * inverse, inverse


def norm_pull(upstream, scaled, inverse, gain):
    weighted = upstream * gain
    first = jnp.mean(weighted, axis=-1, keepdims=True)
    second = jnp.mean(weighted * scaled, axis=-1, keepdims=True)
    return inverse * (weighted - first - scaled * second)


def step_kernel(
    lines,
    lat, cot, counts, assign, pre_gain, pre_shift, b_out, mid_gain, mid_shift, b_down, bias_in,
    w_query, w_key, w_value, w_out, w_up, w_down,
    y_out, gx_out, grads_out, vec_out,
    wc, wr, bias, xb, dy, n1, n2, lhs, rhs, fa, fb, vec,
    csend, crecv, ysend, yrecv, xsend, xrecv, zsend, zrecv, gathered, vrecv, vz,
    load_sem, own_sem, out_sem,
    gc_s, gc_r, gy_s, gy_r, gx_s, gx_r, ga_s, ga_r, gb_s, gb_r, bias_s, bias_r,
    c_s, c_r, y_s, y_r, x_s, x_r, z_s, z_r, az_s, az_r, ax_s, ax_r, v_s, v_r,
):
    length, width = xb.shape
    per = wc.shape[3]
    half = width // 2
    piece = half // lines
    scaling = 1.0 / math.sqrt(HEAD)
    dp = lax.axis_index("dp")
    me = lax.axis_index("tensor")
    px, rz = lax.rem(dp, 2), lax.div(dp, 2)
    core, yy = lax.rem(me, 2), lax.div(me, 2)
    t_core, t_y, t_diag = me + 1 - 2 * core, me + 2 - 4 * yy, 3 - me
    to_core, to_y, to_diag = {"tensor": t_core}, {"tensor": t_y}, {"tensor": t_diag}
    to_x = {"dp": dp + 1 - 2 * px}

    def to_z(offset):
        return {"dp": lax.rem(rz + offset, lines) * 2 + px}

    def remote(src, dst, send, recv, target):
        return pltpu.make_async_remote_copy(
            src_ref=src, dst_ref=dst, send_sem=send, recv_sem=recv, device_id=target, device_id_type=MESH
        )

    loads = [
        pltpu.make_async_copy(lat, xb, load_sem.at[0]),
        pltpu.make_async_copy(cot, dy, load_sem.at[1]),
        pltpu.make_async_copy(bias_in, bias.at[me], load_sem.at[2]),
    ]
    for copy in loads:
        copy.start()
    barrier = pltpu.get_barrier_semaphore()
    for target in [to_core, to_y, to_diag, to_x] + [to_z(i) for i in range(1, lines)]:
        pl.semaphore_signal(barrier, inc=1, device_id=target, device_id_type=MESH)
    pl.semaphore_wait(barrier, 3 + lines)

    shards = [
        (w_query, wc.at[0]), (w_key, wc.at[1]), (w_value, wc.at[2]),
        (w_out, wr.at[0]), (w_up, wc.at[3]), (w_down, wr.at[1]),
    ]

    def part(ref, index):
        size = ref.shape[0] // 2
        return ref.at[aligned(index * size, size)]

    def own_copy(w):
        return pltpu.make_async_copy(shards[w][0], shards[w][1].at[me], own_sem.at[w])

    def core_copy(w, who):
        return remote(shards[w][0], shards[w][1].at[who], gc_s.at[w], gc_r.at[w], to_core)

    def y_copy(w, who):
        return remote(part(shards[w][0], px), part(shards[w][1].at[who], px), gy_s.at[w], gy_r.at[w], to_y)

    def x_copy(w, which):
        ref = part(shards[w][1].at[t_y], which)
        return remote(ref, ref, gx_s.at[w], gx_r.at[w], to_x)

    def a_copy(w, who):
        ref = part(shards[w][1].at[who], px)
        return remote(ref, ref, ga_s.at[w], ga_r.at[w], to_core)

    def b_copy(w, who):
        ref = part(shards[w][1].at[who], 1 - px)
        return remote(ref, ref, gb_s.at[w], gb_r.at[w], to_core)

    for w in range(6):
        y_copy(w, me).start()
        core_copy(w, me).start()
        own_copy(w).start()
    loads[2].wait()
    for i, target in enumerate((to_core, to_y, to_diag)):
        remote(bias.at[me], bias.at[me], bias_s.at[i], bias_r.at[i], target).start()

    def gather_first(w):
        y_copy(w, t_y).wait_recv()
        x_copy(w, px).start()
        a_copy(w, t_y).start()

    def gather_second(w):
        x_copy(w, 1 - px).wait_recv()
        b_copy(w, t_y).start()

    def gather_near(w):
        own_copy(w).wait()
        core_copy(w, t_core).wait_recv()

    def gather_far(w):
        a_copy(w, t_diag).wait_recv()
        b_copy(w, t_diag).wait_recv()

    loads[0].wait()
    loads[1].wait()
    total = jnp.sum(jnp.where(assign[...] == dp, counts[...], 0).astype(F32), axis=-1, keepdims=True)
    live = (me.astype(F32) < total).astype(F32)
    vec[...] = jnp.zeros_like(vec)

    def add_vec(row, values):
        vec[row : row + 1, :] += jnp.sum(values, axis=0, keepdims=True)

    @pl.loop(0, length // ROWS)
    def _(i):
        rows = aligned(i * ROWS, ROWS)
        scaled, _ = row_stats(xb[rows, :].astype(F32))
        normed = scaled * pre_gain[...] + pre_shift[...]
        n1[rows, :] = normed.astype(BF16)
        lhs[3, :, rows] = normed.T.astype(BF16)
        grad = dy[rows, :].astype(F32) * live
        dy[rows, :] = grad.astype(BF16)
        lhs[0, :, rows] = grad.T.astype(BF16)
        add_vec(5, grad)

    for i, who in enumerate((t_core, t_y, t_diag)):
        remote(bias.at[who], bias.at[who], bias_s.at[i], bias_r.at[i], to_core).wait_recv()

    def project(who):
        columns = aligned(who * per, per)

        @pl.loop(0, 3)
        def _(i):
            value = dot(n1[...], wc[i, who]) + bias[who, pl.ds(i, 1), :]
            rhs[3 + i, :, columns] = value.astype(BF16)

    def probabilities(rows, columns):
        scores = dot_nt(rhs[3, rows, columns], rhs[4, :, columns]) * scaling
        exponent = jnp.exp(scores - jnp.max(scores, axis=-1, keepdims=True))
        return exponent / jnp.sum(exponent, axis=-1, keepdims=True)

    QROWS = length // 2

    def attend(head):
        columns = aligned(head * HEAD, HEAD)

        @pl.loop(0, 2)
        def _(i):
            rows = aligned(i * QROWS, QROWS)
            probs = probabilities(rows, columns).astype(BF16)
            rhs[2, rows, columns] = dot(probs, rhs[5, :, columns]).astype(BF16)

    for w in range(3):
        gather_near(w)
    for who in (me, t_core):
        project(who)
    gather_first(0)
    for i, who in enumerate((me, t_core)):
        attend(2 * who)
        attend(2 * who + 1)
        gather_first(i + 1)
        gather_second(i)
    gather_first(3)
    gather_second(2)
    for w in range(3):
        gather_far(w)
    for who in (t_y, t_diag):
        project(who)
    gather_first(4)
    gather_second(3)
    for who in (t_y, t_diag):
        attend(2 * who)
        attend(2 * who + 1)

    gather_near(3)
    gather_far(3)

    @pl.loop(0, 4)
    def _(i):
        columns = aligned(i * per, per)
        value = dot(rhs[2], wr[0, :, :, columns].reshape(width, per))
        fa[:, columns] = xb[:, columns].astype(F32) + (value + b_out[:, columns])

    gather_first(5)
    gather_second(4)

    @pl.loop(0, length // ROWS)
    def _(i):
        rows = aligned(i * ROWS, ROWS)
        scaled, _ = row_stats(fa[rows, :])
        normed = scaled * mid_gain[...] + mid_shift[...]
        n2[rows, :] = normed.astype(BF16)
        lhs[1, :, rows] = normed.T.astype(BF16)

    gather_near(4)
    gather_far(4)

    @pl.loop(0, 4)
    def _(i):
        columns = aligned(i * per, per)
        up = dot(n2[...], wc[3, i]) + bias[i, 3:4, :]
        root = math.sqrt(2.0 / math.pi)
        square = up * up
        curve = jnp.tanh(root * up * (1.0 + 0.044715 * square))
        outer = 0.5 * (1.0 + curve)
        rhs[0, :, columns] = (up * outer).astype(BF16)
        slope = root * (1.0 + 3 * 0.044715 * square)
        fb[:, columns] = outer + 0.5 * up * (1.0 - curve * curve) * slope

    def place(k):
        early = k < 6
        late = k - 6
        which = jnp.where(early, lax.div(k, 2), 3 + lax.rem(late + 6, 3))
        side = jnp.where(early, lax.rem(k, 2), jnp.where(late >= 3, 1, 0))
        return which, side, jnp.minimum(which, 3)

    def block_of(which, side, who):
        return rhs[which, :, aligned(who * per + side * BLOCK, BLOCK)]

    def c_copy(k):
        return remote(csend.at[k], crecv.at[k], c_s.at[k], c_r.at[k], to_core)

    def yg_copy(k):
        return remote(ysend.at[k], yrecv.at[k], y_s.at[k], y_r.at[k], to_y)

    def xg_copy(k):
        return remote(xsend.at[k], xrecv.at[k], x_s.at[k], x_r.at[k], to_x)

    def z_copy(k, offset):
        peer = lax.rem(rz + offset, lines)
        return remote(
            zsend.at[k, aligned(peer * piece, piece)], zrecv.at[k, offset - 1], z_s.at[k], z_r.at[k], to_z(offset)
        )

    def z_all(k):
        return remote(zrecv.at[k], zrecv.at[k], z_s.at[k], z_r.at[k], to_x)

    def az_copy(k, offset):
        ref = gathered.at[k, aligned(px * half + rz * piece, piece)]
        return remote(ref, ref, az_s.at[k], az_r.at[k], to_z(offset))

    def az_all(k):
        return remote(zrecv.at[k], zrecv.at[k], az_s.at[k], az_r.at[k], to_x)

    def ax_copy(k, which):
        ref = gathered.at[k, aligned(which * half, half)]
        return remote(ref, ref, ax_s.at[k], ax_r.at[k], to_x)

    def out_copy(k):
        return pltpu.make_async_copy(gathered.at[k], grads_out.at[k], out_sem.at[k])

    def stage0(k):
        which, side, left = place(k)
        pair = jnp.concatenate(
            [block_of(which, side, 1 - core), block_of(which, side, 3 - core)], axis=1
        )

        @pl.loop(0, 2)
        def _(i):
            rows = aligned(i * half, half)
            value = dot(lhs[left, rows, :], pair).astype(BF16)
            csend[k, 0, rows, :] = value[:, :BLOCK]
            csend[k, 1, rows, :] = value[:, BLOCK:]

        c_copy(k).start()

    def stage1(k):
        which, side, left = place(k)
        c_copy(k).wait_recv()
        value = dot(lhs[left], block_of(which, side, t_y))
        ysend[k] = (value + crecv[k, 1 - yy].astype(F32)).astype(BF16)
        yg_copy(k).start()

    def stage2(k):
        which, side, left = place(k)
        yg_copy(k).wait_recv()
        rows = aligned((1 - px) * half, half)
        value = dot(lhs[left, rows, :], block_of(which, side, me))
        value = value + crecv[k, yy, rows, :].astype(F32) + yrecv[k, rows, :].astype(F32)
        xsend[k] = value.astype(BF16)
        xg_copy(k).start()

    def stage3(k):
        which, side, left = place(k)
        rows = aligned(px * half, half)
        value = dot(lhs[left, rows, :], block_of(which, side, me))
        value = value + crecv[k, yy, rows, :].astype(F32) + yrecv[k, rows, :].astype(F32)
        xg_copy(k).wait_recv()
        zsend[k] = (value + xrecv[k].astype(F32)).astype(BF16)
        for offset in range(1, lines):
            z_copy(k, offset).start()

    def stage4(k):
        z_all(k).wait_recv()
        value = zsend[k, aligned(rz * piece, piece), :].astype(F32)
        for offset in range(1, lines):
            value = value + zrecv[k, offset - 1].astype(F32)
        gathered[k, aligned(px * half + rz * piece, piece), :] = value.astype(BF16)
        for offset in range(1, lines):
            az_copy(k, offset).start()

    def stage5(k):
        az_all(k).wait_recv()
        ax_copy(k, px).start()

    def stage6(k):
        ax_copy(k, 1 - px).wait_recv()
        out_copy(k).start()

    def v_copy(i, target):
        return remote(vec.at[pl.ds(16 * i, 16)], vrecv.at[i], v_s.at[i], v_r.at[i], target)

    def vz_copy(offset):
        ref = vz.at[rz]
        return remote(ref, ref, v_s.at[3], v_r.at[3], to_z(offset))

    def vz_all():
        ref = vz.at[pl.ds(0, lines - 1)]
        return remote(ref, ref, v_s.at[3], v_r.at[3], to_x)

    def piece_out():
        @pl.loop(0, 4)
        def _(i):
            columns = aligned(i * per, per)
            value = dot(rhs[0], wr[1, :, :, columns].reshape(width, per))
            value = fa[:, columns] + (value + b_down[:, columns])
            n1[:, columns] = (value * live).astype(BF16)

        pltpu.make_async_copy(n1, y_out, load_sem.at[3]).start()

        @pl.loop(0, 4)
        def _(i):
            columns = aligned(i * per, per)
            value = (dot_nt(dy[...], wr[1, i]) * fb[:, columns]).astype(BF16)
            rhs[1, :, columns] = value
            vec[8:9, columns] = jnp.sum(value.astype(F32), axis=0, keepdims=True)

    def piece_mid():
        @pl.loop(0, 4)
        def _(i):
            rows = aligned(i * per, per)
            value = dot_nt(rhs[1, :, :per], wc[3, 0, rows, :])
            for who in range(1, 4):
                value = value + dot_nt(rhs[1, :, who * per : (who + 1) * per], wc[3, who, rows, :])
            fb[:, rows] = value

        @pl.loop(0, length // ROWS)
        def _(i):
            rows = aligned(i * ROWS, ROWS)
            scaled, inverse = row_stats(fa[rows, :])
            up = fb[rows, :]
            add_vec(3, up * scaled)
            add_vec(4, up)
            value = dy[rows, :].astype(F32) + norm_pull(up, scaled, inverse, mid_gain[...])
            fb[rows, :] = value
            low = value.astype(BF16)
            n2[rows, :] = low
            lhs[2, :, rows] = value.T.astype(BF16)
            add_vec(2, low.astype(F32))

    def piece_mixed():
        pltpu.make_async_copy(n1, y_out, load_sem.at[3]).wait()

        @pl.loop(0, 4)
        def _(i):
            columns = aligned(i * per, per)
            n1[:, columns] = dot_nt(n2[...], wr[0, i]).astype(BF16)

    def piece_head(head):
        columns = aligned(head * HEAD, HEAD)
        queries, keys, values = rhs[3, :, columns], rhs[4, :, columns], rhs[5, :, columns]
        grad_queries = []
        grad_keys = jnp.zeros((length, HEAD), F32)
        grad_values = jnp.zeros((length, HEAD), F32)
        for i in range(2):
            rows = slice(i * QROWS, (i + 1) * QROWS)
            probs = probabilities(rows, columns)
            upstream = n1[rows, columns]
            grad_values = grad_values + dot_tn(probs.astype(BF16), upstream)
            grad_probs = dot_nt(upstream, values)
            inner = jnp.sum(probs * grad_probs, axis=-1, keepdims=True)
            grad_scores = (probs * (grad_probs - inner)).astype(BF16)
            grad_keys = grad_keys + dot_tn(grad_scores, rhs[3, rows, columns])
            grad_queries.append((dot(grad_scores, keys) * scaling).astype(BF16))
        grad_queries = jnp.concatenate(grad_queries, axis=0)
        grad_values = grad_values.astype(BF16)
        rhs[3, :, columns] = grad_queries
        rhs[4, :, columns] = (grad_keys * scaling).astype(BF16)
        rhs[5, :, columns] = grad_values
        vec[6:7, columns] = jnp.sum(grad_queries.astype(F32), axis=0, keepdims=True)
        vec[7:8, columns] = jnp.sum(grad_values.astype(F32), axis=0, keepdims=True)

    def piece_input():
        @pl.loop(0, 4)
        def _(i):
            rows = aligned(i * per, per)
            fa[:, rows] = jnp.zeros((length, per), F32)

            @pl.loop(0, 3)
            def _(m):
                value = fa[:, rows]
                for who in range(4):
                    value = value + dot_nt(rhs[3 + m, :, who * per : (who + 1) * per], wc[m, who, rows, :])
                fa[:, rows] = value

    def piece_last():
        @pl.loop(0, length // ROWS)
        def _(i):
            rows = aligned(i * ROWS, ROWS)
            scaled, inverse = row_stats(xb[rows, :].astype(F32))
            up = fa[rows, :]
            add_vec(0, up * scaled)
            add_vec(1, up)
            fa[rows, :] = fb[rows, :] + norm_pull(up, scaled, inverse, pre_gain[...])

        pltpu.make_async_copy(fa, gx_out, load_sem.at[4]).start()
        v_copy(0, to_core).start()

    stages = [stage0, stage1, stage2, stage3, stage4, stage5, stage6]

    @pl.loop(0, CHUNKS + len(stages) - 1)
    def _(tick):
        @pl.when(tick == 0)
        def _():
            gather_second(5)
            gather_near(5)
            gather_far(5)
            piece_out()

        pl.when(tick == 1)(piece_mid)
        pl.when(tick == 2)(piece_mixed)

        @pl.when((tick >= 2) & (tick < 10))
        def _():
            order = tick - 2
            piece_head(2 * lax.rem(order, 4) + lax.div(order, 4))

        pl.when(tick == 10)(piece_input)
        pl.when(tick == 11)(piece_last)
        for number, stage in enumerate(stages):
            k = tick - number

            @pl.when((k >= 0) & (k < CHUNKS))
            def _():
                stage(jnp.clip(k, 0, CHUNKS - 1))

        for i, target in ((0, to_y), (1, to_x)):
            @pl.when(tick == 12 + i)
            def _():
                v_copy(i, to_core).wait_recv()
                vec[16 * (i + 1) : 16 * (i + 2), :] = vec[16 * i : 16 * (i + 1), :] + vrecv[i]
                v_copy(i + 1, target).start()

        @pl.when(tick == 14)
        def _():
            v_copy(2, to_x).wait_recv()
            vz[rz] = vec[32:48, :] + vrecv[2]
            for offset in range(1, lines):
                vz_copy(offset).start()

        @pl.when(tick == 16)
        def _():
            vz_all().wait_recv()
            value = vz[0]
            for i in range(1, lines):
                value = value + vz[i]
            vec_out[...] = value

    for w in range(6):
        y_copy(w, me).wait_send()
        core_copy(w, me).wait_send()
        x_copy(w, px).wait_send()
        a_copy(w, t_y).wait_send()
        b_copy(w, t_y).wait_send()
    for i in range(3):
        remote(bias.at[me], bias.at[me], bias_s.at[i], bias_r.at[i], to_core).wait_send()
        v_copy(i, to_core).wait_send()
    vz_all().wait_send()

    @pl.loop(0, CHUNKS)
    def _(k):
        c_copy(k).wait_send()
        yg_copy(k).wait_send()
        xg_copy(k).wait_send()
        z_all(k).wait_send()
        az_all(k).wait_send()
        ax_copy(k, px).wait_send()
        out_copy(k).wait()

    pltpu.make_async_copy(fa, gx_out, load_sem.at[4]).wait()


def shards_of(
    lines,
    latents, cotangent, counts, assign, pre_gain, pre_shift, w_query, b_query, w_key, w_value, b_value,
    w_out, b_out, mid_gain, mid_shift, w_up, b_up, w_down, b_down,
):
    _, length, width = latents.shape
    per = w_query.shape[1]
    half = width // 2
    line = lambda a: a.reshape(1, -1)
    zero = jnp.zeros_like(b_query)
    bias_in = jnp.stack([b_query, zero, b_value, b_up, zero, zero, zero, zero])
    anywhere = pl.BlockSpec(memory_space=pl.ANY)
    inside = pl.BlockSpec(memory_space=pltpu.VMEM)
    dma = pltpu.SemaphoreType.DMA
    y_out, gx_out, grads, sums = pl.pallas_call(
        partial(step_kernel, lines),
        out_shape=(
            jax.ShapeDtypeStruct((length, width), BF16),
            jax.ShapeDtypeStruct((length, width), F32),
            jax.ShapeDtypeStruct((CHUNKS, width, BLOCK), BF16),
            jax.ShapeDtypeStruct((16, width), F32),
        ),
        in_specs=[anywhere] * 2 + [inside] * 8 + [anywhere] * 7,
        out_specs=(anywhere, anywhere, anywhere, inside),
        scratch_shapes=[
            pltpu.VMEM((4, 4, width, per), BF16),
            pltpu.VMEM((2, 4, per, width), BF16),
            pltpu.VMEM((4, 8, per), F32),
            pltpu.VMEM((length, width), BF16),
            pltpu.VMEM((length, width), BF16),
            pltpu.VMEM((length, width), BF16),
            pltpu.VMEM((length, width), BF16),
            pltpu.VMEM((4, width, length), BF16),
            pltpu.VMEM((6, length, width), BF16),
            pltpu.VMEM((length, width), F32),
            pltpu.VMEM((length, width), F32),
            pltpu.VMEM((48, width), F32),
            pltpu.VMEM((CHUNKS, 2, width, BLOCK), BF16),
            pltpu.VMEM((CHUNKS, 2, width, BLOCK), BF16),
            pltpu.VMEM((CHUNKS, width, BLOCK), BF16),
            pltpu.VMEM((CHUNKS, width, BLOCK), BF16),
            pltpu.VMEM((CHUNKS, half, BLOCK), BF16),
            pltpu.VMEM((CHUNKS, half, BLOCK), BF16),
            pltpu.VMEM((CHUNKS, half, BLOCK), BF16),
            pltpu.VMEM((CHUNKS, lines - 1, half // lines, BLOCK), BF16),
            pltpu.VMEM((CHUNKS, width, BLOCK), BF16),
            pltpu.VMEM((3, 16, width), F32),
            pltpu.VMEM((lines, 16, width), F32),
            dma((5,)), dma((6,)), dma((CHUNKS,)),
        ]
        + [dma((6,))] * 10
        + [dma((3,))] * 2
        + [dma((CHUNKS,))] * 12
        + [dma((4,))] * 2,
        compiler_params=pltpu.CompilerParams(
            collective_id=0, has_side_effects=True, vmem_limit_bytes=67043328
        ),
    )(
        latents.reshape(length, width), cotangent.reshape(length, width), line(counts), line(assign),
        line(pre_gain), line(pre_shift), line(b_out), line(mid_gain), line(mid_shift), line(b_down), bias_in,
        w_query, w_key, w_value, w_out, w_up, w_down,
    )

    def pick(first, second):
        return jnp.concatenate([grads[first], grads[second]], axis=1).astype(F32)

    mine = lax.dynamic_slice_in_dim(sums[6:9], lax.axis_index("tensor") * per, per, axis=1)
    return (
        y_out.reshape(latents.shape),
        gx_out.reshape(latents.shape),
        sums[0], sums[1],
        pick(6, 9), mine[0], pick(7, 10), pick(8, 11), mine[1],
        pick(4, 5).T, sums[2], sums[3], sums[4],
        pick(2, 3), mine[2], pick(0, 1).T, sums[5],
    )


def solution(mesh):
    assert mesh.shape["tensor"] == 4
    return jax.shard_map(
        partial(shards_of, mesh.shape["dp"] // 2),
        mesh=mesh,
        in_specs=(
            P(("dp", "tensor"), None, None),
            P(("dp", "tensor"), None, None),
            P(),
            P(),
            P(),
            P(),
            P(None, "tensor"),
            P("tensor"),
            P(None, "tensor"),
            P(None, "tensor"),
            P("tensor"),
            P("tensor", None),
            P(),
            P(),
            P(),
            P(None, "tensor"),
            P("tensor"),
            P("tensor", None),
            P(),
        ),
        out_specs=(
            P(("dp", "tensor"), None, None),
            P(("dp", "tensor"), None, None),
            P(),
            P(),
            P(None, "tensor"),
            P("tensor"),
            P(None, "tensor"),
            P(None, "tensor"),
            P("tensor"),
            P("tensor", None),
            P(),
            P(),
            P(),
            P(None, "tensor"),
            P("tensor"),
            P("tensor", None),
            P(),
        ),
        check_vma=False,
    )
```

time: 426 us -> 216 us (0.51); the launches traced: 419 us -> 215 us
  waiting for transfers between devices: 213 us -> 0 us
  Pallas kernels: 0 us -> 198 us
  matrix products: 72 us -> 0 us
  blocking collectives: 49.2 us -> 0 us
  local copies, waits for them, and re-layouts: 45.9 us -> 12.2 us
  other arithmetic: 23.4 us -> 4.23 us
  between operations: 15.5 us -> 0.69 us
    pallas_call x0 -> x1, Pallas kernels: none -> 198 us  [shards_of(): pl.pallas_call(partial(step_kernel, lines), out_shape=(jax.ShapeDtypeStru...]
    all_gather x1 -> x0, waiting for transfers between devices: 76.6 us -> none  [shards(): lax.all_gather(columns, 'tensor', axis=0, tiled=False)]
    psum x1 -> x0, waiting for transfers between devices: 73.5 us -> none  [total(): return lax.psum(part, 'dp')[0].astype(f32)]
    dot_general x23 -> x0, matrix products: 66.8 us -> none  [the longest x18 44 us: dot(): lax.dot_general(left, right, (dims, ((), ())), preferred_element_type=f32)]
    reduce_scatter x2 -> x0, waiting for transfers between devices: 62.8 us -> none  [total(): part = lax.psum_scatter(stacked, 'tensor', scatter_dimension=0, tiled=True)]
    psum x1 -> x0, blocking collectives: 42.9 us -> none  [shards(): lax.psum(jnp.stack([col(gn1 * scaled), col(gn1), col(ga), col(gn2 * scale...]
    another operation x7 -> x3, local copies, waits for them, and re-layouts: 16.7 us -> 1.33 us  [shards_of(): bias_in = jnp.stack([b_query, zero, b_value, b_up, zero, zero, zero, zero])]
    another operation x3 -> x0, other arithmetic: 9.87 us -> none  [the longest x2 9.86 us: total(): jnp.stack([p.astype(bf16).reshape(tensor, per, width) for p in parts], ax...]
  transfers between devices with their start and end apart: 4 -> 0, of which waited for: 4 -> 0; matrix products, arithmetic and copies ran while one was open for 18% -> 0% of each run, Pallas kernels for 0% -> 0%
where the time goes in v2:
time: 216 us; the launch traced here: 215 us
  Pallas kernels  198 us (92%)
  local copies, waits for them, and re-layouts  12.2 us (6%)
  other arithmetic  4.23 us (2%)
    pallas_call x1, Pallas kernels, shards_of(): pl.pallas_call(partial(step_kernel, lines), out_shape=(jax.ShapeDtypeStru...  198 us
    unnamed x8, local copies, waits for them, and re-layouts  4.91 us

profile of v2, /device:TPU:0, one launch (start us, length us, event | category | flops | bytes accessed | tf_op | source)
XLA Modules:
  0.0 215.4 jit_solution(17051028085838619085)
XLA Ops:
  0.7 1.3 stack.19.bias_in
  2.0 198.3 %shard_map.314 = (bf16[512,1024]{1,0:T(8,128)(2,1)}, f32[512,1024]{1,0:T(8,128)}, bf16[12,1024,128]{2,1,0:T(8,128)(2,1)}, f32[16,1024]{1,0:T(8,128)}) custom-call(bf16[512,1024]{1,0:T(8,128)(2,1)} %bitcast.54, bf16[512,1024]{1,0:T(8,128)(2,1)} %bitcast.55, s32[1,16]{1,0:T(1,128)} %bitcast.74, s32[1,16]{1,0:T(1,128)} %bitcast.75, f32[1,1024]{1,0:T(1,128)} %bitcast.62, ...), custom_call_target="tpu_custom_call" | custom-call | tf_op jit(solution)/shard_map/pallas_call | solution.py:552
  200.3 0.8 slice.70
  201.1 1.7 fusion
  202.8 0.6 fusion.1
  203.5 2.8 %slice_bitcast_fusion.1 = (bf16[1024,128]{1,0:T(8,128)(2,1)S(1)}, bf16[1024,128]{1,0:T(8,128)(2,1)S(1)}, bf16[1024,128]{1,0:T(8,128)(2,1)S(1)}, bf16[1024,128]{1...) fusion(bf16[12,1024,128]{2,1,0:T(8,128)(2,1)} %get-tuple-element.24), kind=kLoop, calls=%fused_computation.7 | loop fusion | bytes 6291456 | tf_op jit(solution)/shard_map/squeeze | solution.py:602
  206.3 0.1 convert_bitcast_fusion
  206.4 1.3 copy.37
  207.7 1.3 copy.36
  209.0 0.0 copy-start.1
  209.0 2.6 %maximum_convert_fusion.2 = (f32[1024,256]{1,0:T(8,128)}, f32[1024,256]{1,0:T(8,128)}) fusion(bf16[1024,128]{1,0:T(8,128)(2,1)} %get-tuple-element.48, bf16[1024,128]{1,0:T(8,128)(2,1)} %get-tuple-element.49, bf16[1024,128]{1,0:T(8,128)(2,1)S(1)} %get-tuple-element.44, bf16[1024,128]{1,0:T(8,128)(2,1)} %get-tuple-element.45), kind=kLoop, calls=%fused_computation.4 | loop fusion | flops 2097152 | bytes 3145728 | tf_op jit(solution)/shard_map/convert_element_type | solution.py:602
  211.7 0.0 copy-start
  211.7 1.5 maximum_convert_fusion
  213.1 0.0 copy-done.1
  213.1 1.0 copy.40
  214.1 0.0 copy-done
  214.1 1.3 copy.41
  (2 shorter events, 0.0 us)
Async XLA Ops:
  209.0 4.1 %copy-start.1 = (bf16[512,1024]{1,0:T(8,128)(2,1)S(1)}, bf16[512,1024]{1,0:T(8,128)(2,1)}, u32[]{:S(2)}) copy-start(bf16[512,1024]{1,0:T(8,128)(2,1)} %get-tuple-element.21) | copy-start | bytes 3145732
  211.7 2.4 %copy-start = (f32[512,1024]{1,0:T(8,128)S(1)}, f32[512,1024]{1,0:T(8,128)}, u32[]{:S(2)}) copy-start(f32[512,1024]{1,0:T(8,128)} %get-tuple-element.22) | copy-start | bytes 6291460

commit v3 on v2

--- a/solution.py
+++ b/solution.py
@@ -50,7 +50,7 @@
 
 def step_kernel(
     lines,
-    lat, cot, counts, assign, pre_gain, pre_shift, b_out, mid_gain, mid_shift, b_down, bias_in,
+    lat, cot, counts, assign, pre_gain, pre_shift, b_out, mid_gain, mid_shift, b_down, b_query, b_value, b_up,
     w_query, w_key, w_value, w_out, w_up, w_down,
     y_out, gx_out, grads_out, vec_out,
     wc, wr, bias, xb, dy, n1, n2, lhs, rhs, fa, fb, vec,
@@ -83,7 +83,9 @@
     loads = [
         pltpu.make_async_copy(lat, xb, load_sem.at[0]),
         pltpu.make_async_copy(cot, dy, load_sem.at[1]),
-        pltpu.make_async_copy(bias_in, bias.at[me], load_sem.at[2]),
+        pltpu.make_async_copy(b_query, bias.at[me, 0:1], load_sem.at[2]),
+        pltpu.make_async_copy(b_value, bias.at[me, 1:2], load_sem.at[5]),
+        pltpu.make_async_copy(b_up, bias.at[me, 2:3], load_sem.at[6]),
     ]
     for copy in loads:
         copy.start()
@@ -122,16 +124,23 @@
         ref = part(shards[w][1].at[who], 1 - px)
         return remote(ref, ref, gb_s.at[w], gb_r.at[w], to_core)
 
+    def bias_copy(i, who, target):
+        ref = bias.at[who, 0:3]
+        return remote(ref, ref, bias_s.at[i], bias_r.at[i], target)
+
+    y_copy(0, me).start()
     for w in range(6):
-        y_copy(w, me).start()
         core_copy(w, me).start()
         own_copy(w).start()
-    loads[2].wait()
+    for copy in loads[2:]:
+        copy.wait()
     for i, target in enumerate((to_core, to_y, to_diag)):
-        remote(bias.at[me], bias.at[me], bias_s.at[i], bias_r.at[i], target).start()
+        bias_copy(i, me, target).start()
 
     def gather_first(w):
         y_copy(w, t_y).wait_recv()
+        if w + 2 < 6:
+            y_copy(w + 2, me).start()
         x_copy(w, px).start()
         a_copy(w, t_y).start()
 
@@ -152,6 +161,8 @@
     total = jnp.sum(jnp.where(assign[...] == dp, counts[...], 0).astype(F32), axis=-1, keepdims=True)
     live = (me.astype(F32) < total).astype(F32)
     vec[...] = jnp.zeros_like(vec)
+    for who in range(4):
+        bias[who, 3:4, :] = jnp.zeros((1, per), F32)
 
     def add_vec(row, values):
         vec[row : row + 1, :] += jnp.sum(values, axis=0, keepdims=True)
@@ -168,15 +179,19 @@
         lhs[0, :, rows] = grad.T.astype(BF16)
         add_vec(5, grad)
 
+        @pl.when(i == 1)
+        def _():
+            y_copy(1, me).start()
+
     for i, who in enumerate((t_core, t_y, t_diag)):
-        remote(bias.at[who], bias.at[who], bias_s.at[i], bias_r.at[i], to_core).wait_recv()
+        bias_copy(i, who, to_core).wait_recv()
 
     def project(who):
         columns = aligned(who * per, per)
 
         @pl.loop(0, 3)
         def _(i):
-            value = dot(n1[...], wc[i, who]) + bias[who, pl.ds(i, 1), :]
+            value = dot(n1[...], wc[i, who]) + bias[who, pl.ds(jnp.where(i == 1, 3, lax.div(i, 2)), 1), :]
             rhs[3 + i, :, columns] = value.astype(BF16)
 
     def probabilities(rows, columns):
@@ -243,7 +258,7 @@
     @pl.loop(0, 4)
     def _(i):
         columns = aligned(i * per, per)
-        up = dot(n2[...], wc[3, i]) + bias[i, 3:4, :]
+        up = dot(n2[...], wc[3, i]) + bias[i, 2:3, :]
         root = math.sqrt(2.0 / math.pi)
         square = up * up
         curve = jnp.tanh(root * up * (1.0 + 0.044715 * square))
@@ -463,7 +478,9 @@
 
     stages = [stage0, stage1, stage2, stage3, stage4, stage5, stage6]
 
-    @pl.loop(0, CHUNKS + len(stages) - 1)
+    lags = [0, 1, 3, 4, 5, 6, 7]
+
+    @pl.loop(0, CHUNKS + lags[-1])
     def _(tick):
         @pl.when(tick == 0)
         def _():
@@ -482,8 +499,8 @@
 
         pl.when(tick == 10)(piece_input)
         pl.when(tick == 11)(piece_last)
-        for number, stage in enumerate(stages):
-            k = tick - number
+        for lag, stage in zip(lags, stages):
+            k = tick - lag
 
             @pl.when((k >= 0) & (k < CHUNKS))
             def _():
@@ -518,7 +535,7 @@
         a_copy(w, t_y).wait_send()
         b_copy(w, t_y).wait_send()
     for i in range(3):
-        remote(bias.at[me], bias.at[me], bias_s.at[i], bias_r.at[i], to_core).wait_send()
+        bias_copy(i, me, to_core).wait_send()
         v_copy(i, to_core).wait_send()
     vz_all().wait_send()
 
@@ -535,6 +552,53 @@
     pltpu.make_async_copy(fa, gx_out, load_sem.at[4]).wait()
 
 
+PAIRS = ((6, 9), (7, 10), (8, 11), (2, 3), (4, 5), (0, 1))
+
+
+def finish_kernel(
+    grads, y_in, gx_in, sums,
+    y_out, gx_out, g_query, g_key, g_value, g_up, g_out, g_down,
+    v0, v1, v2, v3, v4, v5, b0, b1, b2,
+    low, high, tall, yb, gb, in_sem, out_sem,
+):
+    per = high.shape[2]
+    me = lax.axis_index("tensor")
+    loads = [
+        pltpu.make_async_copy(grads.at[k], low.at[m, i], in_sem.at[2 * m + i])
+        for m, pair in enumerate(PAIRS)
+        for i, k in enumerate(pair)
+    ]
+    loads += [pltpu.make_async_copy(y_in, yb, in_sem.at[12]), pltpu.make_async_copy(gx_in, gb, in_sem.at[13])]
+    stores = [
+        pltpu.make_async_copy(high.at[m], out, out_sem.at[m])
+        for m, out in enumerate((g_query, g_key, g_value, g_up))
+    ]
+    stores += [pltpu.make_async_copy(tall.at[m], out, out_sem.at[4 + m]) for m, out in enumerate((g_out, g_down))]
+    stores += [pltpu.make_async_copy(yb, y_out, out_sem.at[6]), pltpu.make_async_copy(gb, gx_out, out_sem.at[7])]
+    for copy in loads[12:]:
+        copy.start()
+    for copy in loads[:12]:
+        copy.start()
+    for out, row in ((v0, 0), (v1, 1), (v2, 2), (v3, 3), (v4, 4), (v5, 5)):
+        out[...] = sums[row : row + 1, :]
+    for out, row in ((b0, 6), (b1, 7), (b2, 8)):
+        out[...] = sums[row : row + 1, aligned(me * per, per)]
+    for i in range(2):
+        loads[12 + i].wait()
+        stores[6 + i].start()
+    for m in range(6):
+        loads[2 * m].wait()
+        loads[2 * m + 1].wait()
+        for i in range(2):
+            if m < 4:
+                high[m, :, i * BLOCK : (i + 1) * BLOCK] = low[m, i].astype(F32)
+            else:
+                tall[m - 4, i * BLOCK : (i + 1) * BLOCK, :] = low[m, i].astype(F32).T
+        stores[m].start()
+    for copy in stores:
+        copy.wait()
+
+
 def shards_of(
     lines,
     latents, cotangent, counts, assign, pre_gain, pre_shift, w_query, b_query, w_key, w_value, b_value,
@@ -544,8 +608,6 @@
     per = w_query.shape[1]
     half = width // 2
     line = lambda a: a.reshape(1, -1)
-    zero = jnp.zeros_like(b_query)
-    bias_in = jnp.stack([b_query, zero, b_value, b_up, zero, zero, zero, zero])
     anywhere = pl.BlockSpec(memory_space=pl.ANY)
     inside = pl.BlockSpec(memory_space=pltpu.VMEM)
     dma = pltpu.SemaphoreType.DMA
@@ -557,7 +619,7 @@
             jax.ShapeDtypeStruct((CHUNKS, width, BLOCK), BF16),
             jax.ShapeDtypeStruct((16, width), F32),
         ),
-        in_specs=[anywhere] * 2 + [inside] * 8 + [anywhere] * 7,
+        in_specs=[anywhere] * 2 + [inside] * 8 + [anywhere] * 9,
         out_specs=(anywhere, anywhere, anywhere, inside),
         scratch_shapes=[
             pltpu.VMEM((4, 4, width, per), BF16),
@@ -583,7 +645,7 @@
             pltpu.VMEM((CHUNKS, width, BLOCK), BF16),
             pltpu.VMEM((3, 16, width), F32),
             pltpu.VMEM((lines, 16, width), F32),
-            dma((5,)), dma((6,)), dma((CHUNKS,)),
+            dma((7,)), dma((6,)), dma((CHUNKS,)),
         ]
         + [dma((6,))] * 10
         + [dma((3,))] * 2
@@ -594,21 +656,39 @@
         ),
     )(
         latents.reshape(length, width), cotangent.reshape(length, width), line(counts), line(assign),
-        line(pre_gain), line(pre_shift), line(b_out), line(mid_gain), line(mid_shift), line(b_down), bias_in,
+        line(pre_gain), line(pre_shift), line(b_out), line(mid_gain), line(mid_shift), line(b_down),
+        line(b_query), line(b_value), line(b_up),
         w_query, w_key, w_value, w_out, w_up, w_down,
     )
 
-    def pick(first, second):
-        return jnp.concatenate([grads[first], grads[second]], axis=1).astype(F32)
-
-    mine = lax.dynamic_slice_in_dim(sums[6:9], lax.axis_index("tensor") * per, per, axis=1)
+    full = jax.ShapeDtypeStruct((1, width), F32)
+    own = jax.ShapeDtypeStruct((1, per), F32)
+    wide = jax.ShapeDtypeStruct((width, per), F32)
+    flat = jax.ShapeDtypeStruct((per, width), F32)
+    results = pl.pallas_call(
+        finish_kernel,
+        out_shape=(
+            jax.ShapeDtypeStruct((length, width), BF16),
+            jax.ShapeDtypeStruct((length, width), F32),
+            *[wide] * 4, *[flat] * 2, *[full] * 6, *[own] * 3,
+        ),
+        in_specs=[anywhere] * 3 + [inside],
+        out_specs=(*[anywhere] * 8, *[inside] * 9),
+        scratch_shapes=[
+            pltpu.VMEM((6, 2, width, BLOCK), BF16),
+            pltpu.VMEM((4, width, per), F32),
+            pltpu.VMEM((2, per, width), F32),
+            pltpu.VMEM((length, width), BF16),
+            pltpu.VMEM((length, width), F32),
+            dma((14,)), dma((8,)),
+        ],
+        compiler_params=pltpu.CompilerParams(vmem_limit_bytes=67043328),
+    )(grads, y_out, gx_out, sums)
+    y_out, gx_out, g_query, g_key, g_value, g_up, g_out, g_down = results[:8]
+    v0, v1, v2, v3, v4, v5, b0, b1, b2 = [a.reshape(-1) for a in results[8:]]
     return (
-        y_out.reshape(latents.shape),
-        gx_out.reshape(latents.shape),
-        sums[0], sums[1],
-        pick(6, 9), mine[0], pick(7, 10), pick(8, 11), mine[1],
-        pick(4, 5).T, sums[2], sums[3], sums[4],
-        pick(2, 3), mine[2], pick(0, 1).T, sums[5],
+        y_out.reshape(latents.shape), gx_out.reshape(latents.shape),
+        v0, v1, g_query, b0, g_key, g_value, b1, g_out, v2, v3, v4, g_up, b2, g_down, v5,
     )
 
 

time: 216 us -> 175 us (0.81)
  Pallas kernels: 198 us -> 174 us
  local copies, waits for them, and re-layouts: 12.2 us -> 0 us
  other arithmetic: 4.23 us -> 0 us
    pallas_call x1, Pallas kernels: 198 us -> 167 us  [shards_of(): pl.pallas_call(partial(step_kernel, lines), out_shape=(jax.ShapeDtypeStru...]
    pallas_call x0 -> x1, Pallas kernels: none -> 6.86 us  [shards_of(): pl.pallas_call(finish_kernel, out_shape=(jax.ShapeDtypeStruct((length, wi...]
    unnamed x8 -> x0, local copies, waits for them, and re-layouts: 4.91 us -> none
    convert_element_type x2 -> x0, other arithmetic: 4.1 us -> none  [pick(): return jnp.concatenate([grads[first], grads[second]], axis=1).astype(F32)]
    slice x3 -> x0, local copies, waits for them, and re-layouts: 3.19 us -> none  [the longest x1 1.7 us: shards_of(): sums[5]]
    squeeze x1 -> x0, local copies, waits for them, and re-layouts: 2.81 us -> none  [pick(): return jnp.concatenate([grads[first], grads[second]], axis=1).astype(F32)]
where the time goes in v3:
time: 175 us
  Pallas kernels  174 us (99%)
    pallas_call x1, Pallas kernels, shards_of(): pl.pallas_call(partial(step_kernel, lines), out_shape=(jax.ShapeDtypeStru...  167 us
    pallas_call x1, Pallas kernels, shards_of(): pl.pallas_call(finish_kernel, out_shape=(jax.ShapeDtypeStruct((length, wi...  6.86 us

profile of v3, /device:TPU:0, one launch (start us, length us, event | category | flops | bytes accessed | tf_op | source)
XLA Modules:
  0.0 174.7 jit_solution(15171040243398795076)
XLA Ops:
  0.7 167.2 %shard_map.314 = (bf16[512,1024]{1,0:T(8,128)(2,1)}, f32[512,1024]{1,0:T(8,128)}, bf16[12,1024,128]{2,1,0:T(8,128)(2,1)}, f32[16,1024]{1,0:T(8,128)}) custom-call(bf16[512,1024]{1,0:T(8,128)(2,1)} %bitcast.24, bf16[512,1024]{1,0:T(8,128)(2,1)} %bitcast.25, s32[1,16]{1,0:T(1,128)} %bitcast.35, s32[1,16]{1,0:T(1,128)} %bitcast.36, f32[1,1024]{1,0:T(1,128)} %bitcast.26, ...), custom_call_target="tpu_custom_call" | custom-call | tf_op jit(solution)/shard_map/pallas_call | solution.py:614
  167.8 6.9 %shard_map.315 = (bf16[512,1024]{1,0:T(8,128)(2,1)}, f32[512,1024]{1,0:T(8,128)}, f32[1024,256]{1,0:T(8,128)}, f32[1024,256]{1,0:T(8,128)}, f32[1024,256]{1,0:T(...) custom-call(bf16[12,1024,128]{2,1,0:T(8,128)(2,1)} %get-tuple-elemen, ...), custom_call_target="tpu_custom_call" | custom-call | tf_op jit(solution)/shard_map/pallas_call | solution.py:668

commit v4 on v3

--- a/solution.py
+++ b/solution.py
@@ -13,6 +13,8 @@
 CHUNKS = 12
 BLOCK = 128
 ROWS = 128
+LAGS = (0, 1, 3, 5, 7, 9, 11)
+WEAVE = dict(up=1, down=3, mid=5, mixed=7, even=8, odd=12, out=16, input=18, last=22)
 F32 = jnp.float32
 BF16 = jnp.bfloat16
 MESH = pl.DeviceIdType.MESH
@@ -49,7 +51,7 @@
 
 
 def step_kernel(
-    lines,
+    lines, split, lags, weave,
     lat, cot, counts, assign, pre_gain, pre_shift, b_out, mid_gain, mid_shift, b_down, b_query, b_value, b_up,
     w_query, w_key, w_value, w_out, w_up, w_down,
     y_out, gx_out, grads_out, vec_out,
@@ -61,7 +63,9 @@
 ):
     length, width = xb.shape
     per = wc.shape[3]
-    half = width // 2
+    chunks = CHUNKS * split
+    tall = width // split
+    half = tall // 2
     piece = half // lines
     scaling = 1.0 / math.sqrt(HEAD)
     dp = lax.axis_index("dp")
@@ -268,11 +272,12 @@
         fb[:, columns] = outer + 0.5 * up * (1.0 - curve * curve) * slope
 
     def place(k):
-        early = k < 6
-        late = k - 6
-        which = jnp.where(early, lax.div(k, 2), 3 + lax.rem(late + 6, 3))
-        side = jnp.where(early, lax.rem(k, 2), jnp.where(late >= 3, 1, 0))
-        return which, side, jnp.minimum(which, 3)
+        base = lax.div(k, split)
+        late = base - 6
+        early = late < 0
+        which = jnp.where(early, lax.div(base, 2), 3 + lax.rem(late + 6, 3))
+        side = jnp.where(early, lax.rem(base, 2), jnp.where(late >= 3, 1, 0))
+        return which, side, jnp.minimum(which, 3), lax.rem(k, split) * tall
 
     def block_of(which, side, who):
         return rhs[which, :, aligned(who * per + side * BLOCK, BLOCK)]
@@ -307,44 +312,45 @@
         return remote(ref, ref, ax_s.at[k], ax_r.at[k], to_x)
 
     def out_copy(k):
-        return pltpu.make_async_copy(gathered.at[k], grads_out.at[k], out_sem.at[k])
+        target = grads_out.at[lax.div(k, split), aligned(lax.rem(k, split) * tall, tall)]
+        return pltpu.make_async_copy(gathered.at[k], target, out_sem.at[k])
 
     def stage0(k):
-        which, side, left = place(k)
+        which, side, left, start = place(k)
         pair = jnp.concatenate(
             [block_of(which, side, 1 - core), block_of(which, side, 3 - core)], axis=1
         )
-
-        @pl.loop(0, 2)
+        size = tall // (2 // split)
+
+        @pl.loop(0, 2 // split)
         def _(i):
-            rows = aligned(i * half, half)
-            value = dot(lhs[left, rows, :], pair).astype(BF16)
+            value = dot(lhs[left, aligned(start + i * size, size), :], pair).astype(BF16)
+            rows = aligned(i * size, size)
             csend[k, 0, rows, :] = value[:, :BLOCK]
             csend[k, 1, rows, :] = value[:, BLOCK:]
 
         c_copy(k).start()
 
     def stage1(k):
-        which, side, left = place(k)
+        which, side, left, start = place(k)
         c_copy(k).wait_recv()
-        value = dot(lhs[left], block_of(which, side, t_y))
+        value = dot(lhs[left, aligned(start, tall), :], block_of(which, side, t_y))
         ysend[k] = (value + crecv[k, 1 - yy].astype(F32)).astype(BF16)
         yg_copy(k).start()
 
+    def near_sum(k, index):
+        which, side, left, start = place(k)
+        rows = aligned(index * half, half)
+        value = dot(lhs[left, aligned(start + index * half, half), :], block_of(which, side, me))
+        return value + crecv[k, yy, rows, :].astype(F32) + yrecv[k, rows, :].astype(F32)
+
     def stage2(k):
-        which, side, left = place(k)
         yg_copy(k).wait_recv()
-        rows = aligned((1 - px) * half, half)
-        value = dot(lhs[left, rows, :], block_of(which, side, me))
-        value = value + crecv[k, yy, rows, :].astype(F32) + yrecv[k, rows, :].astype(F32)
-        xsend[k] = value.astype(BF16)
+        xsend[k] = near_sum(k, 1 - px).astype(BF16)
         xg_copy(k).start()
 
     def stage3(k):
-        which, side, left = place(k)
-        rows = aligned(px * half, half)
-        value = dot(lhs[left, rows, :], block_of(which, side, me))
-        value = value + crecv[k, yy, rows, :].astype(F32) + yrecv[k, rows, :].astype(F32)
+        value = near_sum(k, px)
         xg_copy(k).wait_recv()
         zsend[k] = (value + xrecv[k].astype(F32)).astype(BF16)
         for offset in range(1, lines):
@@ -378,53 +384,42 @@
         ref = vz.at[pl.ds(0, lines - 1)]
         return remote(ref, ref, v_s.at[3], v_r.at[3], to_x)
 
-    def piece_out():
-        @pl.loop(0, 4)
-        def _(i):
-            columns = aligned(i * per, per)
-            value = dot(rhs[0], wr[1, :, :, columns].reshape(width, per))
-            value = fa[:, columns] + (value + b_down[:, columns])
-            n1[:, columns] = (value * live).astype(BF16)
-
-        pltpu.make_async_copy(n1, y_out, load_sem.at[3]).start()
-
-        @pl.loop(0, 4)
-        def _(i):
-            columns = aligned(i * per, per)
-            value = (dot_nt(dy[...], wr[1, i]) * fb[:, columns]).astype(BF16)
-            rhs[1, :, columns] = value
-            vec[8:9, columns] = jnp.sum(value.astype(F32), axis=0, keepdims=True)
-
-    def piece_mid():
-        @pl.loop(0, 4)
-        def _(i):
-            rows = aligned(i * per, per)
-            value = dot_nt(rhs[1, :, :per], wc[3, 0, rows, :])
-            for who in range(1, 4):
-                value = value + dot_nt(rhs[1, :, who * per : (who + 1) * per], wc[3, who, rows, :])
-            fb[:, rows] = value
-
-        @pl.loop(0, length // ROWS)
-        def _(i):
-            rows = aligned(i * ROWS, ROWS)
-            scaled, inverse = row_stats(fa[rows, :])
-            up = fb[rows, :]
-            add_vec(3, up * scaled)
-            add_vec(4, up)
-            value = dy[rows, :].astype(F32) + norm_pull(up, scaled, inverse, mid_gain[...])
-            fb[rows, :] = value
-            low = value.astype(BF16)
-            n2[rows, :] = low
-            lhs[2, :, rows] = value.T.astype(BF16)
-            add_vec(2, low.astype(F32))
-
-    def piece_mixed():
-        pltpu.make_async_copy(n1, y_out, load_sem.at[3]).wait()
-
-        @pl.loop(0, 4)
-        def _(i):
-            columns = aligned(i * per, per)
-            n1[:, columns] = dot_nt(n2[...], wr[0, i]).astype(BF16)
+    def piece_out(i):
+        columns = aligned(i * per, per)
+        value = dot(rhs[0], wr[1, :, :, columns].reshape(width, per))
+        value = fa[:, columns] + (value + b_down[:, columns])
+        low = (value * live).astype(BF16)
+        n2[:, columns] = low
+
+    def piece_up(i):
+        columns = aligned(i * per, per)
+        value = (dot_nt(dy[...], wr[1, i]) * fb[:, columns]).astype(BF16)
+        rhs[1, :, columns] = value
+        vec[8:9, columns] = jnp.sum(value.astype(F32), axis=0, keepdims=True)
+
+    def piece_down(i):
+        rows = aligned(i * per, per)
+        value = dot_nt(rhs[1, :, :per], wc[3, 0, rows, :])
+        for who in range(1, 4):
+            value = value + dot_nt(rhs[1, :, who * per : (who + 1) * per], wc[3, who, rows, :])
+        fb[:, rows] = value
+
+    def piece_mid(i):
+        rows = aligned(i * ROWS, ROWS)
+        scaled, inverse = row_stats(fa[rows, :])
+        up = fb[rows, :]
+        add_vec(3, up * scaled)
+        add_vec(4, up)
+        value = dy[rows, :].astype(F32) + norm_pull(up, scaled, inverse, mid_gain[...])
+        fb[rows, :] = value
+        low = value.astype(BF16)
+        n2[rows, :] = low
+        lhs[2, :, rows] = value.T.astype(BF16)
+        add_vec(2, low.astype(F32))
+
+    def piece_mixed(i):
+        columns = aligned(i * per, per)
+        n1[:, columns] = dot_nt(n2[...], wr[0, i]).astype(BF16)
 
     def piece_head(head):
         columns = aligned(head * HEAD, HEAD)
@@ -450,77 +445,91 @@
         vec[6:7, columns] = jnp.sum(grad_queries.astype(F32), axis=0, keepdims=True)
         vec[7:8, columns] = jnp.sum(grad_values.astype(F32), axis=0, keepdims=True)
 
-    def piece_input():
-        @pl.loop(0, 4)
-        def _(i):
-            rows = aligned(i * per, per)
-            fa[:, rows] = jnp.zeros((length, per), F32)
-
-            @pl.loop(0, 3)
-            def _(m):
-                value = fa[:, rows]
-                for who in range(4):
-                    value = value + dot_nt(rhs[3 + m, :, who * per : (who + 1) * per], wc[m, who, rows, :])
-                fa[:, rows] = value
-
-    def piece_last():
-        @pl.loop(0, length // ROWS)
-        def _(i):
-            rows = aligned(i * ROWS, ROWS)
-            scaled, inverse = row_stats(xb[rows, :].astype(F32))
-            up = fa[rows, :]
-            add_vec(0, up * scaled)
-            add_vec(1, up)
-            fa[rows, :] = fb[rows, :] + norm_pull(up, scaled, inverse, pre_gain[...])
-
-        pltpu.make_async_copy(fa, gx_out, load_sem.at[4]).start()
-        v_copy(0, to_core).start()
-
-    stages = [stage0, stage1, stage2, stage3, stage4, stage5, stage6]
-
-    lags = [0, 1, 3, 4, 5, 6, 7]
-
-    @pl.loop(0, CHUNKS + lags[-1])
-    def _(tick):
-        @pl.when(tick == 0)
+    def piece_input(i):
+        rows = aligned(i * per, per)
+        n1_part = jnp.zeros((length, per), F32)
+        for m in range(3):
+            for who in range(4):
+                n1_part = n1_part + dot_nt(rhs[3 + m, :, who * per : (who + 1) * per], wc[m, who, rows, :])
+        fa[:, rows] = n1_part
+
+    def piece_last(i):
+        rows = aligned(i * ROWS, ROWS)
+        scaled, inverse = row_stats(xb[rows, :].astype(F32))
+        up = fa[rows, :]
+        add_vec(0, up * scaled)
+        add_vec(1, up)
+        fa[rows, :] = fb[rows, :] + norm_pull(up, scaled, inverse, pre_gain[...])
+
+    def y_store():
+        return pltpu.make_async_copy(n2, y_out, load_sem.at[3])
+
+    def gx_store():
+        return pltpu.make_async_copy(fa, gx_out, load_sem.at[4])
+
+    def compute(step):
+        def during(first, count, size, run):
+            @pl.when((step >= first) & (step < first + count))
+            def _():
+                @pl.loop(0, size)
+                def _(i):
+                    run((step - first) * size + i)
+
+        @pl.when(step == weave["up"])
         def _():
             gather_second(5)
             gather_near(5)
             gather_far(5)
-            piece_out()
-
-        pl.when(tick == 1)(piece_mid)
-        pl.when(tick == 2)(piece_mixed)
-
-        @pl.when((tick >= 2) & (tick < 10))
+
+        during(weave["up"], 2, 2, piece_up)
+        during(weave["down"], 2, 2, piece_down)
+        during(weave["mid"], 2, length // ROWS // 2, piece_mid)
+        during(weave["mixed"], 1, 4, piece_mixed)
+        during(weave["even"], 4, 1, lambda i: piece_head(2 * i))
+        during(weave["odd"], 4, 1, lambda i: piece_head(2 * i + 1))
+        during(weave["out"], 2, 2, piece_out)
+        pl.when(step == weave["out"] + 1)(lambda: y_store().start())
+        during(weave["input"], 4, 1, piece_input)
+        during(weave["last"], 2, length // ROWS // 2, piece_last)
+
+        @pl.when(step == weave["last"] + 1)
         def _():
-            order = tick - 2
-            piece_head(2 * lax.rem(order, 4) + lax.div(order, 4))
-
-        pl.when(tick == 10)(piece_input)
-        pl.when(tick == 11)(piece_last)
+            gx_store().start()
+            v_copy(0, to_core).start()
+
+    stages = [stage0, stage1, stage2, stage3, stage4, stage5, stage6]
+
+    fine = 2 // split
+    after = (weave["last"] + 1) // fine + 1
+
+    @pl.loop(0, chunks + lags[-1])
+    def _(tick):
         for lag, stage in zip(lags, stages):
             k = tick - lag
 
-            @pl.when((k >= 0) & (k < CHUNKS))
+            @pl.when((k >= 0) & (k < chunks))
             def _():
-                stage(jnp.clip(k, 0, CHUNKS - 1))
+                stage(jnp.clip(k, 0, chunks - 1))
+
+        @pl.loop(0, fine)
+        def _(i):
+            compute(tick * fine + i)
 
         for i, target in ((0, to_y), (1, to_x)):
-            @pl.when(tick == 12 + i)
+            @pl.when(tick == after + i)
             def _():
                 v_copy(i, to_core).wait_recv()
                 vec[16 * (i + 1) : 16 * (i + 2), :] = vec[16 * i : 16 * (i + 1), :] + vrecv[i]
                 v_copy(i + 1, target).start()
 
-        @pl.when(tick == 14)
+        @pl.when(tick == after + 2)
         def _():
             v_copy(2, to_x).wait_recv()
             vz[rz] = vec[32:48, :] + vrecv[2]
             for offset in range(1, lines):
                 vz_copy(offset).start()
 
-        @pl.when(tick == 16)
+        @pl.when(tick == after + 4)
         def _():
             vz_all().wait_recv()
             value = vz[0]
@@ -539,7 +548,7 @@
         v_copy(i, to_core).wait_send()
     vz_all().wait_send()
 
-    @pl.loop(0, CHUNKS)
+    @pl.loop(0, chunks)
     def _(k):
         c_copy(k).wait_send()
         yg_copy(k).wait_send()
@@ -549,7 +558,8 @@
         ax_copy(k, px).wait_send()
         out_copy(k).wait()
 
-    pltpu.make_async_copy(fa, gx_out, load_sem.at[4]).wait()
+    y_store().wait()
+    gx_store().wait()
 
 
 PAIRS = ((6, 9), (7, 10), (8, 11), (2, 3), (4, 5), (0, 1))
@@ -606,13 +616,16 @@
 ):
     _, length, width = latents.shape
     per = w_query.shape[1]
-    half = width // 2
+    split = 2 if lines <= 16 else 1
+    chunks = CHUNKS * split
+    tall = width // split
+    half = tall // 2
     line = lambda a: a.reshape(1, -1)
     anywhere = pl.BlockSpec(memory_space=pl.ANY)
     inside = pl.BlockSpec(memory_space=pltpu.VMEM)
     dma = pltpu.SemaphoreType.DMA
     y_out, gx_out, grads, sums = pl.pallas_call(
-        partial(step_kernel, lines),
+        partial(step_kernel, lines, split, LAGS, WEAVE),
         out_shape=(
             jax.ShapeDtypeStruct((length, width), BF16),
             jax.ShapeDtypeStruct((length, width), F32),
@@ -634,22 +647,22 @@
             pltpu.VMEM((length, width), F32),
             pltpu.VMEM((length, width), F32),
             pltpu.VMEM((48, width), F32),
-            pltpu.VMEM((CHUNKS, 2, width, BLOCK), BF16),
-            pltpu.VMEM((CHUNKS, 2, width, BLOCK), BF16),
-            pltpu.VMEM((CHUNKS, width, BLOCK), BF16),
-            pltpu.VMEM((CHUNKS, width, BLOCK), BF16),
-            pltpu.VMEM((CHUNKS, half, BLOCK), BF16),
-            pltpu.VMEM((CHUNKS, half, BLOCK), BF16),
-            pltpu.VMEM((CHUNKS, half, BLOCK), BF16),
-            pltpu.VMEM((CHUNKS, lines - 1, half // lines, BLOCK), BF16),
-            pltpu.VMEM((CHUNKS, width, BLOCK), BF16),
+            pltpu.VMEM((chunks, 2, tall, BLOCK), BF16),
+            pltpu.VMEM((chunks, 2, tall, BLOCK), BF16),
+            pltpu.VMEM((chunks, tall, BLOCK), BF16),
+            pltpu.VMEM((chunks, tall, BLOCK), BF16),
+            pltpu.VMEM((chunks, half, BLOCK), BF16),
+            pltpu.VMEM((chunks, half, BLOCK), BF16),
+            pltpu.VMEM((chunks, half, BLOCK), BF16),
+            pltpu.VMEM((chunks, lines - 1, half // lines, BLOCK), BF16),
+            pltpu.VMEM((chunks, tall, BLOCK), BF16),
             pltpu.VMEM((3, 16, width), F32),
             pltpu.VMEM((lines, 16, width), F32),
-            dma((7,)), dma((6,)), dma((CHUNKS,)),
+            dma((7,)), dma((6,)), dma((chunks,)),
         ]
         + [dma((6,))] * 10
         + [dma((3,))] * 2
-        + [dma((CHUNKS,))] * 12
+        + [dma((chunks,))] * 12
         + [dma((4,))] * 2,
         compiler_params=pltpu.CompilerParams(
             collective_id=0, has_side_effects=True, vmem_limit_bytes=67043328

time: 175 us -> 164 us (0.937)
  Pallas kernels: 174 us -> 163 us
    pallas_call x1, Pallas kernels: 167 us -> 156 us  [shards_of(): pl.pallas_call(partial(step_kernel, lines, split, LAGS, WEAVE), out_shape...]
where the time goes in v4:
time: 164 us
  Pallas kernels  163 us (99%)
    pallas_call x1, Pallas kernels, shards_of(): pl.pallas_call(partial(step_kernel, lines, split, LAGS, WEAVE), out_shape...  156 us
    pallas_call x1, Pallas kernels, shards_of(): pl.pallas_call(finish_kernel, out_shape=(jax.ShapeDtypeStruct((length, wi...  6.86 us

profile of v4, /device:TPU:0, one launch (start us, length us, event | category | flops | bytes accessed | tf_op | source)
XLA Modules:
  0.0 164.2 jit_solution(14855546894099851456)
XLA Ops:
  0.7 156.5 %shard_map.314 = (bf16[512,1024]{1,0:T(8,128)(2,1)}, f32[512,1024]{1,0:T(8,128)}, bf16[12,1024,128]{2,1,0:T(8,128)(2,1)}, f32[16,1024]{1,0:T(8,128)}) custom-call(bf16[512,1024]{1,0:T(8,128)(2,1)} %bitcast.24, bf16[512,1024]{1,0:T(8,128)(2,1)} %bitcast.25, s32[1,16]{1,0:T(1,128)} %bitcast.35, s32[1,16]{1,0:T(1,128)} %bitcast.36, f32[1,1024]{1,0:T(1,128)} %bitcast.26, ...), custom_call_target="tpu_custom_call" | custom-call | tf_op jit(solution)/shard_map/pallas_call | solution.py:627
  157.1 6.9 %shard_map.315 = (bf16[512,1024]{1,0:T(8,128)(2,1)}, f32[512,1024]{1,0:T(8,128)}, f32[1024,256]{1,0:T(8,128)}, f32[1024,256]{1,0:T(8,128)}, f32[1024,256]{1,0:T(...) custom-call(bf16[12,1024,128]{2,1,0:T(8,128)(2,1)} %get-tuple-elemen, ...), custom_call_target="tpu_custom_call" | custom-call | tf_op jit(solution)/shard_map/pallas_call | solution.py:681

commit v5 on v4

--- a/solution.py
+++ b/solution.py
@@ -13,7 +13,8 @@
 CHUNKS = 12
 BLOCK = 128
 ROWS = 128
-LAGS = (0, 1, 3, 5, 7, 9, 11)
+RING = 8
+LAGS = {1: (0, 1, 2, 3, 4, 5, 6, 7), 2: (0, 1, 3, 5, 7, 9, 11, 13)}
 WEAVE = dict(up=1, down=3, mid=5, mixed=7, even=8, odd=12, out=16, input=18, last=22)
 F32 = jnp.float32
 BF16 = jnp.bfloat16
@@ -56,10 +57,10 @@
     w_query, w_key, w_value, w_out, w_up, w_down,
     y_out, gx_out, grads_out, vec_out,
     wc, wr, bias, xb, dy, n1, n2, lhs, rhs, fa, fb, vec,
-    csend, crecv, ysend, yrecv, xsend, xrecv, zsend, zrecv, gathered, vrecv, vz,
+    near, csend, crecv, ysend, yrecv, xsend, xrecv, zsend, zrecv, gathered, vrecv, vz,
     load_sem, own_sem, out_sem,
-    gc_s, gc_r, gy_s, gy_r, gx_s, gx_r, ga_s, ga_r, gb_s, gb_r, bias_s, bias_r,
-    c_s, c_r, y_s, y_r, x_s, x_r, z_s, z_r, az_s, az_r, ax_s, ax_r, v_s, v_r,
+    gc_s, gc_r, gy_s, gy_r, gx_s, gx_r, gp_s, gp_r, gxx_s, gxx_r, gpp_s, gpp_r, ga_s, ga_r, bias_s, bias_r,
+    c_s, c_r, y_s, y_r, x_s, x_r, z_s, z_r, az_s, az_r, bz_s, bz_r, ax_s, ax_r, v_s, v_r,
 ):
     length, width = xb.shape
     per = wc.shape[3]
@@ -75,6 +76,8 @@
     t_core, t_y, t_diag = me + 1 - 2 * core, me + 2 - 4 * yy, 3 - me
     to_core, to_y, to_diag = {"tensor": t_core}, {"tensor": t_y}, {"tensor": t_diag}
     to_x = {"dp": dp + 1 - 2 * px}
+    qz = lax.rem(rz, 2)
+    to_pair = {"dp": (rz + 1 - 2 * qz) * 2 + px}
 
     def to_z(offset):
         return {"dp": lax.rem(rz + offset, lines) * 2 + px}
@@ -103,30 +106,39 @@
         (w_out, wr.at[0]), (w_up, wc.at[3]), (w_down, wr.at[1]),
     ]
 
-    def part(ref, index):
-        size = ref.shape[0] // 2
+    def part(ref, index, count):
+        size = ref.shape[0] // count
         return ref.at[aligned(index * size, size)]
 
     def own_copy(w):
         return pltpu.make_async_copy(shards[w][0], shards[w][1].at[me], own_sem.at[w])
 
     def core_copy(w, who):
-        return remote(shards[w][0], shards[w][1].at[who], gc_s.at[w], gc_r.at[w], to_core)
+        return remote(shards[w][0], shards[w][1].at[who], gc_s.at[0], gc_r.at[w], to_core)
 
     def y_copy(w, who):
-        return remote(part(shards[w][0], px), part(shards[w][1].at[who], px), gy_s.at[w], gy_r.at[w], to_y)
+        mine = 2 * px + qz
+        return remote(part(shards[w][0], mine, 4), part(shards[w][1].at[who], mine, 4), gy_s.at[0], gy_r.at[w], to_y)
 
     def x_copy(w, which):
-        ref = part(shards[w][1].at[t_y], which)
-        return remote(ref, ref, gx_s.at[w], gx_r.at[w], to_x)
-
-    def a_copy(w, who):
-        ref = part(shards[w][1].at[who], px)
-        return remote(ref, ref, ga_s.at[w], ga_r.at[w], to_core)
-
-    def b_copy(w, who):
-        ref = part(shards[w][1].at[who], 1 - px)
-        return remote(ref, ref, gb_s.at[w], gb_r.at[w], to_core)
+        ref = part(shards[w][1].at[t_y], 2 * which + qz, 4)
+        return remote(ref, ref, gx_s.at[0], gx_r.at[w], to_x)
+
+    def p_copy(w, which):
+        ref = part(shards[w][1].at[t_y], 2 * px + which, 4)
+        return remote(ref, ref, gp_s.at[0], gp_r.at[w], to_pair)
+
+    def xx_copy(w, x_part, z_part):
+        ref = part(shards[w][1].at[t_y], 2 * (2 * x_part + z_part), 8)
+        return remote(ref, ref, gxx_s.at[0], gxx_r.at[w], to_x)
+
+    def pp_copy(w, x_part, z_part):
+        ref = part(shards[w][1].at[t_y], 2 * (2 * x_part + z_part) + 1, 8)
+        return remote(ref, ref, gpp_s.at[0], gpp_r.at[w], to_pair)
+
+    def far_copy(w, who):
+        ref = shards[w][1].at[who]
+        return remote(ref, ref, ga_s.at[0], ga_r.at[w], to_core)
 
     def bias_copy(i, who, target):
         ref = bias.at[who, 0:3]
@@ -146,19 +158,25 @@
         if w + 2 < 6:
             y_copy(w + 2, me).start()
         x_copy(w, px).start()
-        a_copy(w, t_y).start()
+        p_copy(w, qz).start()
 
     def gather_second(w):
         x_copy(w, 1 - px).wait_recv()
-        b_copy(w, t_y).start()
+        pp_copy(w, 1 - px, qz).start()
+        p_copy(w, 1 - qz).wait_recv()
+        xx_copy(w, px, 1 - qz).start()
+
+    def gather_third(w):
+        xx_copy(w, 1 - px, 1 - qz).wait_recv()
+        pp_copy(w, 1 - px, 1 - qz).wait_recv()
+        far_copy(w, t_y).start()
 
     def gather_near(w):
         own_copy(w).wait()
         core_copy(w, t_core).wait_recv()
 
     def gather_far(w):
-        a_copy(w, t_diag).wait_recv()
-        b_copy(w, t_diag).wait_recv()
+        far_copy(w, t_diag).wait_recv()
 
     loads[0].wait()
     loads[1].wait()
@@ -175,17 +193,19 @@
     def _(i):
         rows = aligned(i * ROWS, ROWS)
         scaled, _ = row_stats(xb[rows, :].astype(F32))
-        normed = scaled * pre_gain[...] + pre_shift[...]
-        n1[rows, :] = normed.astype(BF16)
-        lhs[3, :, rows] = normed.T.astype(BF16)
-        grad = dy[rows, :].astype(F32) * live
-        dy[rows, :] = grad.astype(BF16)
-        lhs[0, :, rows] = grad.T.astype(BF16)
-        add_vec(5, grad)
-
-        @pl.when(i == 1)
-        def _():
-            y_copy(1, me).start()
+        n1[rows, :] = (scaled * pre_gain[...] + pre_shift[...]).astype(BF16)
+
+    y_copy(1, me).start()
+
+    def prepare(first, count):
+        @pl.loop(first, first + count)
+        def _(i):
+            rows = aligned(i * ROWS, ROWS)
+            lhs[3, :, rows] = n1[rows, :].astype(F32).T.astype(BF16)
+            grad = dy[rows, :].astype(F32) * live
+            dy[rows, :] = grad.astype(BF16)
+            lhs[0, :, rows] = grad.T.astype(BF16)
+            add_vec(5, grad)
 
     for i, who in enumerate((t_core, t_y, t_diag)):
         bias_copy(i, who, to_core).wait_recv()
@@ -199,9 +219,9 @@
             rhs[3 + i, :, columns] = value.astype(BF16)
 
     def probabilities(rows, columns):
-        scores = dot_nt(rhs[3, rows, columns], rhs[4, :, columns]) * scaling
-        exponent = jnp.exp(scores - jnp.max(scores, axis=-1, keepdims=True))
-        return exponent / jnp.sum(exponent, axis=-1, keepdims=True)
+        scores = dot_nt(rhs[3, rows, columns], rhs[4, :, columns]) * (scaling * math.log2(math.e))
+        exponent = jnp.exp2(scores - jnp.max(scores, axis=-1, keepdims=True))
+        return exponent * (1.0 / jnp.sum(exponent, axis=-1, keepdims=True))
 
     QROWS = length // 2
 
@@ -214,27 +234,44 @@
             probs = probabilities(rows, columns).astype(BF16)
             rhs[2, rows, columns] = dot(probs, rhs[5, :, columns]).astype(BF16)
 
+    tiles = length // ROWS
     for w in range(3):
         gather_near(w)
-    for who in (me, t_core):
-        project(who)
+    project(me)
     gather_first(0)
-    for i, who in enumerate((me, t_core)):
-        attend(2 * who)
-        attend(2 * who + 1)
-        gather_first(i + 1)
-        gather_second(i)
+    project(t_core)
+    gather_first(1)
+    prepare(0, tiles // 2)
+    gather_second(0)
+    attend(2 * me)
+    gather_first(2)
+    attend(2 * me + 1)
+    gather_third(0)
+    gather_second(1)
+    attend(2 * t_core)
     gather_first(3)
+    attend(2 * t_core + 1)
+    gather_third(1)
     gather_second(2)
+    prepare(tiles // 2, tiles // 4)
+    gather_first(4)
+    prepare(tiles // 2 + tiles // 4, tiles // 4)
+    gather_third(2)
+    gather_second(3)
     for w in range(3):
         gather_far(w)
-    for who in (t_y, t_diag):
-        project(who)
-    gather_first(4)
-    gather_second(3)
-    for who in (t_y, t_diag):
-        attend(2 * who)
-        attend(2 * who + 1)
+    project(t_y)
+    gather_first(5)
+    gather_third(3)
+    project(t_diag)
+    gather_second(4)
+    attend(2 * t_y)
+    attend(2 * t_y + 1)
+    gather_third(4)
+    gather_second(5)
+    attend(2 * t_diag)
+    attend(2 * t_diag + 1)
+    gather_third(5)
 
     gather_near(3)
     gather_far(3)
@@ -244,9 +281,6 @@
         columns = aligned(i * per, per)
         value = dot(rhs[2], wr[0, :, :, columns].reshape(width, per))
         fa[:, columns] = xb[:, columns].astype(F32) + (value + b_out[:, columns])
-
-    gather_first(5)
-    gather_second(4)
 
     @pl.loop(0, length // ROWS)
     def _(i):
@@ -283,66 +317,76 @@
         return rhs[which, :, aligned(who * per + side * BLOCK, BLOCK)]
 
     def c_copy(k):
-        return remote(csend.at[k], crecv.at[k], c_s.at[k], c_r.at[k], to_core)
+        return remote(csend.at[k], crecv.at[k], c_s.at[0], c_r.at[lax.rem(k, RING)], to_core)
 
     def yg_copy(k):
-        return remote(ysend.at[k], yrecv.at[k], y_s.at[k], y_r.at[k], to_y)
+        return remote(ysend.at[k], yrecv.at[k], y_s.at[0], y_r.at[lax.rem(k, RING)], to_y)
 
     def xg_copy(k):
-        return remote(xsend.at[k], xrecv.at[k], x_s.at[k], x_r.at[k], to_x)
+        return remote(xsend.at[k], xrecv.at[k], x_s.at[0], x_r.at[lax.rem(k, RING)], to_x)
 
     def z_copy(k, offset):
         peer = lax.rem(rz + offset, lines)
         return remote(
-            zsend.at[k, aligned(peer * piece, piece)], zrecv.at[k, offset - 1], z_s.at[k], z_r.at[k], to_z(offset)
+            zsend.at[k, aligned(slot(peer) * piece, piece)], zrecv.at[k, offset - 1], z_s.at[0], z_r.at[lax.rem(k, RING)], to_z(offset)
         )
 
+    def slot(line):
+        return lax.rem(line, 2) * (lines // 2) + lax.div(line, 2)
+
     def z_all(k):
-        return remote(zrecv.at[k], zrecv.at[k], z_s.at[k], z_r.at[k], to_x)
+        return remote(zrecv.at[k], zrecv.at[k], z_s.at[0], z_r.at[lax.rem(k, RING)], to_x)
 
     def az_copy(k, offset):
-        ref = gathered.at[k, aligned(px * half + rz * piece, piece)]
-        return remote(ref, ref, az_s.at[k], az_r.at[k], to_z(offset))
+        peer = lax.rem(lax.div(rz, 2) + offset, lines // 2) * 2 + lax.rem(rz, 2)
+        ref = gathered.at[k, aligned(px * half + slot(rz) * piece, piece)]
+        return remote(ref, ref, az_s.at[0], az_r.at[lax.rem(k, RING)], {"dp": peer * 2 + px})
 
     def az_all(k):
-        return remote(zrecv.at[k], zrecv.at[k], az_s.at[k], az_r.at[k], to_x)
+        ref = zrecv.at[k, pl.ds(0, lines // 2 - 1)]
+        return remote(ref, ref, az_s.at[0], az_r.at[lax.rem(k, RING)], to_x)
+
+    def bz_copy(k, parity):
+        ref = gathered.at[k, aligned(px * half + parity * (half // 2), half // 2)]
+        return remote(ref, ref, bz_s.at[0], bz_r.at[lax.rem(k, RING)], to_pair)
 
     def ax_copy(k, which):
         ref = gathered.at[k, aligned(which * half, half)]
-        return remote(ref, ref, ax_s.at[k], ax_r.at[k], to_x)
+        return remote(ref, ref, ax_s.at[0], ax_r.at[lax.rem(k, RING)], to_x)
 
     def out_copy(k):
         target = grads_out.at[lax.div(k, split), aligned(lax.rem(k, split) * tall, tall)]
-        return pltpu.make_async_copy(gathered.at[k], target, out_sem.at[k])
+        return pltpu.make_async_copy(gathered.at[k], target, out_sem.at[0])
 
     def stage0(k):
         which, side, left, start = place(k)
-        pair = jnp.concatenate(
-            [block_of(which, side, 1 - core), block_of(which, side, 3 - core)], axis=1
-        )
+        kept = lax.rem(k, lags[3] + 1)
         size = tall // (2 // split)
 
         @pl.loop(0, 2 // split)
         def _(i):
-            value = dot(lhs[left, aligned(start + i * size, size), :], pair).astype(BF16)
             rows = aligned(i * size, size)
-            csend[k, 0, rows, :] = value[:, :BLOCK]
-            csend[k, 1, rows, :] = value[:, BLOCK:]
+            block = lhs[left, aligned(start + i * size, size), :]
+            for target, first, second in (
+                (csend.at[k], 1 - core, 3 - core), (near.at[kept], core, core + 2),
+            ):
+                pair = jnp.concatenate([block_of(which, side, first), block_of(which, side, second)], axis=1)
+                value = dot(block, pair).astype(BF16)
+                target[0, rows, :] = value[:, :BLOCK]
+                target[1, rows, :] = value[:, BLOCK:]
 
         c_copy(k).start()
 
     def stage1(k):
-        which, side, left, start = place(k)
         c_copy(k).wait_recv()
-        value = dot(lhs[left, aligned(start, tall), :], block_of(which, side, t_y))
-        ysend[k] = (value + crecv[k, 1 - yy].astype(F32)).astype(BF16)
+        value = near[lax.rem(k, lags[3] + 1), 1 - yy].astype(F32) + crecv[k, 1 - yy].astype(F32)
+        ysend[k] = value.astype(BF16)
         yg_copy(k).start()
 
     def near_sum(k, index):
-        which, side, left, start = place(k)
         rows = aligned(index * half, half)
-        value = dot(lhs[left, aligned(start + index * half, half), :], block_of(which, side, me))
-        return value + crecv[k, yy, rows, :].astype(F32) + yrecv[k, rows, :].astype(F32)
+        value = near[lax.rem(k, lags[3] + 1), yy, rows, :].astype(F32) + crecv[k, yy, rows, :].astype(F32)
+        return value + yrecv[k, rows, :].astype(F32)
 
     def stage2(k):
         yg_copy(k).wait_recv()
@@ -358,18 +402,22 @@
 
     def stage4(k):
         z_all(k).wait_recv()
-        value = zsend[k, aligned(rz * piece, piece), :].astype(F32)
+        value = zsend[k, aligned(slot(rz) * piece, piece), :].astype(F32)
         for offset in range(1, lines):
             value = value + zrecv[k, offset - 1].astype(F32)
-        gathered[k, aligned(px * half + rz * piece, piece), :] = value.astype(BF16)
-        for offset in range(1, lines):
+        gathered[k, aligned(px * half + slot(rz) * piece, piece), :] = value.astype(BF16)
+        for offset in range(1, lines // 2):
             az_copy(k, offset).start()
 
     def stage5(k):
         az_all(k).wait_recv()
+        bz_copy(k, lax.rem(rz, 2)).start()
+
+    def stage6(k):
+        bz_copy(k, 1 - lax.rem(rz, 2)).wait_recv()
         ax_copy(k, px).start()
 
-    def stage6(k):
+    def stage7(k):
         ax_copy(k, 1 - px).wait_recv()
         out_copy(k).start()
 
@@ -477,7 +525,6 @@
 
         @pl.when(step == weave["up"])
         def _():
-            gather_second(5)
             gather_near(5)
             gather_far(5)
 
@@ -497,7 +544,7 @@
             gx_store().start()
             v_copy(0, to_core).start()
 
-    stages = [stage0, stage1, stage2, stage3, stage4, stage5, stage6]
+    stages = [stage0, stage1, stage2, stage3, stage4, stage5, stage6, stage7]
 
     fine = 2 // split
     after = (weave["last"] + 1) // fine + 1
@@ -537,27 +584,33 @@
                 value = value + vz[i]
             vec_out[...] = value
 
-    for w in range(6):
-        y_copy(w, me).wait_send()
-        core_copy(w, me).wait_send()
-        x_copy(w, px).wait_send()
-        a_copy(w, t_y).wait_send()
-        b_copy(w, t_y).wait_send()
     for i in range(3):
         bias_copy(i, me, to_core).wait_send()
         v_copy(i, to_core).wait_send()
     vz_all().wait_send()
 
-    @pl.loop(0, chunks)
-    def _(k):
-        c_copy(k).wait_send()
-        yg_copy(k).wait_send()
-        xg_copy(k).wait_send()
-        z_all(k).wait_send()
-        az_all(k).wait_send()
-        ax_copy(k, px).wait_send()
-        out_copy(k).wait()
-
+    def sent(ref, send, recv):
+        remote(ref, ref, send.at[0], recv.at[0], to_core).wait_send()
+
+    some = wc.at[0, pl.ds(0, 3)]
+    every = wc.at[pl.ds(0, 3), pl.ds(0, 2)]
+    for ref, send, recv in (
+        (every, gc_s, gc_r), (every, ga_s, ga_r),
+        (some.at[:, pl.ds(0, width // 2)], gy_s, gy_r),
+        (some.at[:, pl.ds(0, width // 2)], gx_s, gx_r),
+        (some.at[:, pl.ds(0, width // 2)], gp_s, gp_r),
+        (some.at[:, pl.ds(0, width // 4)], gxx_s, gxx_r),
+        (some.at[:, pl.ds(0, width // 4)], gpp_s, gpp_r),
+    ):
+        sent(ref, send, recv)
+    sent(csend, c_s, c_r)
+    sent(ysend, y_s, y_r)
+    sent(xsend, x_s, x_r)
+    sent(zrecv, z_s, z_r)
+    sent(zrecv.at[:, pl.ds(0, lines // 2 - 1)], az_s, az_r)
+    sent(xsend.at[:, pl.ds(0, half // 2)], bz_s, bz_r)
+    sent(xsend, ax_s, ax_r)
+    pltpu.make_async_copy(gathered, gathered, out_sem.at[0]).wait()
     y_store().wait()
     gx_store().wait()
 
@@ -625,7 +678,7 @@
     inside = pl.BlockSpec(memory_space=pltpu.VMEM)
     dma = pltpu.SemaphoreType.DMA
     y_out, gx_out, grads, sums = pl.pallas_call(
-        partial(step_kernel, lines, split, LAGS, WEAVE),
+        partial(step_kernel, lines, split, LAGS[split], WEAVE),
         out_shape=(
             jax.ShapeDtypeStruct((length, width), BF16),
             jax.ShapeDtypeStruct((length, width), F32),
@@ -647,6 +700,7 @@
             pltpu.VMEM((length, width), F32),
             pltpu.VMEM((length, width), F32),
             pltpu.VMEM((48, width), F32),
+            pltpu.VMEM((LAGS[split][3] + 1, 2, tall, BLOCK), BF16),
             pltpu.VMEM((chunks, 2, tall, BLOCK), BF16),
             pltpu.VMEM((chunks, 2, tall, BLOCK), BF16),
             pltpu.VMEM((chunks, tall, BLOCK), BF16),
@@ -658,11 +712,11 @@
             pltpu.VMEM((chunks, tall, BLOCK), BF16),
             pltpu.VMEM((3, 16, width), F32),
             pltpu.VMEM((lines, 16, width), F32),
-            dma((7,)), dma((6,)), dma((chunks,)),
+            dma((7,)), dma((6,)), dma((1,)),
         ]
-        + [dma((6,))] * 10
+        + [dma((1,)), dma((6,))] * 7
         + [dma((3,))] * 2
-        + [dma((chunks,))] * 12
+        + [dma((1,)), dma((RING,))] * 7
         + [dma((4,))] * 2,
         compiler_params=pltpu.CompilerParams(
             collective_id=0, has_side_effects=True, vmem_limit_bytes=67043328

time: 164 us -> 158 us (0.963)
  Pallas kernels: 163 us -> 157 us
    pallas_call x1, Pallas kernels: 156 us -> 150 us  [shards_of(): pl.pallas_call(partial(step_kernel, lines, split, LAGS[split], WEAVE), ou...]
where the time goes in v5:
time: 158 us
  Pallas kernels  157 us (99%)
    pallas_call x1, Pallas kernels, shards_of(): pl.pallas_call(partial(step_kernel, lines, split, LAGS[split], WEAVE), ou...  150 us
    pallas_call x1, Pallas kernels, shards_of(): pl.pallas_call(finish_kernel, out_shape=(jax.ShapeDtypeStruct((length, wi...  6.86 us

profile of v5, /device:TPU:0, one launch (start us, length us, event | category | flops | bytes accessed | tf_op | source)
XLA Modules:
  0.0 157.6 jit_solution(870282661983592884)
XLA Ops:
  0.7 149.9 %shard_map.314 = (bf16[512,1024]{1,0:T(8,128)(2,1)}, f32[512,1024]{1,0:T(8,128)}, bf16[12,1024,128]{2,1,0:T(8,128)(2,1)}, f32[16,1024]{1,0:T(8,128)}) custom-call(bf16[512,1024]{1,0:T(8,128)(2,1)} %bitcast.24, bf16[512,1024]{1,0:T(8,128)(2,1)} %bitcast.25, s32[1,16]{1,0:T(1,128)} %bitcast.35, s32[1,16]{1,0:T(1,128)} %bitcast.36, f32[1,1024]{1,0:T(1,128)} %bitcast.26, ...), custom_call_target="tpu_custom_call" | custom-call | tf_op jit(solution)/shard_map/pallas_call | solution.py:680
  150.5 6.9 %shard_map.315 = (bf16[512,1024]{1,0:T(8,128)(2,1)}, f32[512,1024]{1,0:T(8,128)}, f32[1024,256]{1,0:T(8,128)}, f32[1024,256]{1,0:T(8,128)}, f32[1024,256]{1,0:T(...) custom-call(bf16[12,1024,128]{2,1,0:T(8,128)(2,1)} %get-tuple-elemen, ...), custom_call_target="tpu_custom_call" | custom-call | tf_op jit(solution)/shard_map/pallas_call | solution.py:735

commit v6 on v5

--- a/solution.py
+++ b/solution.py
@@ -14,8 +14,9 @@
 BLOCK = 128
 ROWS = 128
 RING = 8
+DIRECT = (2, 3, 4)
 LAGS = {1: (0, 1, 2, 3, 4, 5, 6, 7), 2: (0, 1, 3, 5, 7, 9, 11, 13)}
-WEAVE = dict(up=1, down=3, mid=5, mixed=7, even=8, odd=12, out=16, input=18, last=22)
+WEAVE = dict(up=1, down=3, mid=5, mixed=7, even=8, odd=12, out=10, input=16, last=20)
 F32 = jnp.float32
 BF16 = jnp.bfloat16
 MESH = pl.DeviceIdType.MESH
@@ -59,7 +60,7 @@
     wc, wr, bias, xb, dy, n1, n2, lhs, rhs, fa, fb, vec,
     near, csend, crecv, ysend, yrecv, xsend, xrecv, zsend, zrecv, gathered, vrecv, vz,
     load_sem, own_sem, out_sem,
-    gc_s, gc_r, gy_s, gy_r, gx_s, gx_r, gp_s, gp_r, gxx_s, gxx_r, gpp_s, gpp_r, ga_s, ga_r, bias_s, bias_r,
+    gc_s, gc_r, gy_s, gy_r, gyd_s, gyd_r, gx_s, gx_r, gp_s, gp_r, gxx_s, gxx_r, gpp_s, gpp_r, ga_s, ga_r, bias_s, bias_r,
     c_s, c_r, y_s, y_r, x_s, x_r, z_s, z_r, az_s, az_r, bz_s, bz_r, ax_s, ax_r, v_s, v_r,
 ):
     length, width = xb.shape
@@ -120,6 +121,13 @@
         mine = 2 * px + qz
         return remote(part(shards[w][0], mine, 4), part(shards[w][1].at[who], mine, 4), gy_s.at[0], gy_r.at[w], to_y)
 
+    def yd_copy(w, who):
+        other = 3 - 2 * px - qz
+        i = DIRECT.index(w)
+        return remote(
+            part(shards[w][0], other, 4), part(shards[w][1].at[who], other, 4), gyd_s.at[0], gyd_r.at[i], to_y
+        )
+
     def x_copy(w, which):
         ref = part(shards[w][1].at[t_y], 2 * which + qz, 4)
         return remote(ref, ref, gx_s.at[0], gx_r.at[w], to_x)
@@ -159,16 +167,23 @@
             y_copy(w + 2, me).start()
         x_copy(w, px).start()
         p_copy(w, qz).start()
+        if w in DIRECT:
+            yd_copy(w, me).start()
 
     def gather_second(w):
         x_copy(w, 1 - px).wait_recv()
-        pp_copy(w, 1 - px, qz).start()
+        if w not in DIRECT:
+            pp_copy(w, 1 - px, qz).start()
         p_copy(w, 1 - qz).wait_recv()
-        xx_copy(w, px, 1 - qz).start()
+        if w not in DIRECT:
+            xx_copy(w, px, 1 - qz).start()
 
     def gather_third(w):
-        xx_copy(w, 1 - px, 1 - qz).wait_recv()
-        pp_copy(w, 1 - px, 1 - qz).wait_recv()
+        if w in DIRECT:
+            yd_copy(w, t_y).wait_recv()
+        else:
+            xx_copy(w, 1 - px, 1 - qz).wait_recv()
+            pp_copy(w, 1 - px, 1 - qz).wait_recv()
         far_copy(w, t_y).start()
 
     def gather_near(w):
@@ -534,8 +549,8 @@
         during(weave["mixed"], 1, 4, piece_mixed)
         during(weave["even"], 4, 1, lambda i: piece_head(2 * i))
         during(weave["odd"], 4, 1, lambda i: piece_head(2 * i + 1))
-        during(weave["out"], 2, 2, piece_out)
-        pl.when(step == weave["out"] + 1)(lambda: y_store().start())
+        during(weave["out"], 4, 1, piece_out)
+        pl.when(step == weave["out"] + 3)(lambda: y_store().start())
         during(weave["input"], 4, 1, piece_input)
         during(weave["last"], 2, length // ROWS // 2, piece_last)
 
@@ -593,14 +608,15 @@
         remote(ref, ref, send.at[0], recv.at[0], to_core).wait_send()
 
     some = wc.at[0, pl.ds(0, 3)]
+    three = wc.at[0, pl.ds(0, 3), pl.ds(0, width // 8)]
+    six = wc.at[0, pl.ds(0, 3), pl.ds(0, width // 4)]
     every = wc.at[pl.ds(0, 3), pl.ds(0, 2)]
     for ref, send, recv in (
         (every, gc_s, gc_r), (every, ga_s, ga_r),
         (some.at[:, pl.ds(0, width // 2)], gy_s, gy_r),
         (some.at[:, pl.ds(0, width // 2)], gx_s, gx_r),
         (some.at[:, pl.ds(0, width // 2)], gp_s, gp_r),
-        (some.at[:, pl.ds(0, width // 4)], gxx_s, gxx_r),
-        (some.at[:, pl.ds(0, width // 4)], gpp_s, gpp_r),
+        (three, gxx_s, gxx_r), (three, gpp_s, gpp_r), (six, gyd_s, gyd_r),
     ):
         sent(ref, send, recv)
     sent(csend, c_s, c_r)
@@ -714,7 +730,9 @@
             pltpu.VMEM((lines, 16, width), F32),
             dma((7,)), dma((6,)), dma((1,)),
         ]
-        + [dma((1,)), dma((6,))] * 7
+        + [dma((1,)), dma((6,))] * 2
+        + [dma((1,)), dma((3,))]
+        + [dma((1,)), dma((6,))] * 5
         + [dma((3,))] * 2
         + [dma((1,)), dma((RING,))] * 7
         + [dma((4,))] * 2,

time: 158 us -> 154 us (0.975)
  Pallas kernels: 157 us -> 153 us
    pallas_call x1, Pallas kernels: 150 us -> 146 us  [shards_of(): pl.pallas_call(partial(step_kernel, lines, split, LAGS[split], WEAVE), ou...]
where the time goes in v6:
time: 154 us
  Pallas kernels  153 us (99%)
    pallas_call x1, Pallas kernels, shards_of(): pl.pallas_call(partial(step_kernel, lines, split, LAGS[split], WEAVE), ou...  146 us
    pallas_call x1, Pallas kernels, shards_of(): pl.pallas_call(finish_kernel, out_shape=(jax.ShapeDtypeStruct((length, wi...  6.86 us

profile of v6, /device:TPU:0, one launch (start us, length us, event | category | flops | bytes accessed | tf_op | source)
XLA Modules:
  0.0 154.0 jit_solution(7976656932934445914)
XLA Ops:
  0.7 146.3 %shard_map.314 = (bf16[512,1024]{1,0:T(8,128)(2,1)}, f32[512,1024]{1,0:T(8,128)}, bf16[12,1024,128]{2,1,0:T(8,128)(2,1)}, f32[16,1024]{1,0:T(8,128)}) custom-call(bf16[512,1024]{1,0:T(8,128)(2,1)} %bitcast.24, bf16[512,1024]{1,0:T(8,128)(2,1)} %bitcast.25, s32[1,16]{1,0:T(1,128)} %bitcast.35, s32[1,16]{1,0:T(1,128)} %bitcast.36, f32[1,1024]{1,0:T(1,128)} %bitcast.26, ...), custom_call_target="tpu_custom_call" | custom-call | tf_op jit(solution)/shard_map/pallas_call | solution.py:696
  146.9 6.9 %shard_map.315 = (bf16[512,1024]{1,0:T(8,128)(2,1)}, f32[512,1024]{1,0:T(8,128)}, f32[1024,256]{1,0:T(8,128)}, f32[1024,256]{1,0:T(8,128)}, f32[1024,256]{1,0:T(...) custom-call(bf16[12,1024,128]{2,1,0:T(8,128)(2,1)} %get-tuple-elemen, ...), custom_call_target="tpu_custom_call" | custom-call | tf_op jit(solution)/shard_map/pallas_call | solution.py:753

commit v7 on v6

--- a/solution.py
+++ b/solution.py
@@ -15,7 +15,7 @@
 ROWS = 128
 RING = 8
 DIRECT = (2, 3, 4)
-LAGS = {1: (0, 1, 2, 3, 4, 5, 6, 7), 2: (0, 1, 3, 5, 7, 9, 11, 13)}
+LAGS = {1: (0, 1, 2, 3, 4, 5, 6, 7), 2: (0, 1, 3, 4, 6, 8, 10, 12)}
 WEAVE = dict(up=1, down=3, mid=5, mixed=7, even=8, odd=12, out=10, input=16, last=20)
 F32 = jnp.float32
 BF16 = jnp.bfloat16
@@ -252,8 +252,8 @@
     tiles = length // ROWS
     for w in range(3):
         gather_near(w)
+    gather_first(0)
     project(me)
-    gather_first(0)
     project(t_core)
     gather_first(1)
     prepare(0, tiles // 2)

time: 154 us -> 150 us (0.974)
  Pallas kernels: 153 us -> 149 us
    pallas_call x1, Pallas kernels: 146 us -> 142 us  [shards_of(): pl.pallas_call(partial(step_kernel, lines, split, LAGS[split], WEAVE), ou...]
where the time goes in v7:
time: 150 us
  Pallas kernels  149 us (99%)
    pallas_call x1, Pallas kernels, shards_of(): pl.pallas_call(partial(step_kernel, lines, split, LAGS[split], WEAVE), ou...  142 us
    pallas_call x1, Pallas kernels, shards_of(): pl.pallas_call(finish_kernel, out_shape=(jax.ShapeDtypeStruct((length, wi...  6.86 us

profile of v7, /device:TPU:0, one launch (start us, length us, event | category | flops | bytes accessed | tf_op | source)
XLA Modules:
  0.0 149.8 jit_solution(9790300572521428251)
XLA Ops:
  0.7 142.1 %shard_map.314 = (bf16[512,1024]{1,0:T(8,128)(2,1)}, f32[512,1024]{1,0:T(8,128)}, bf16[12,1024,128]{2,1,0:T(8,128)(2,1)}, f32[16,1024]{1,0:T(8,128)}) custom-call(bf16[512,1024]{1,0:T(8,128)(2,1)} %bitcast.24, bf16[512,1024]{1,0:T(8,128)(2,1)} %bitcast.25, s32[1,16]{1,0:T(1,128)} %bitcast.35, s32[1,16]{1,0:T(1,128)} %bitcast.36, f32[1,1024]{1,0:T(1,128)} %bitcast.26, ...), custom_call_target="tpu_custom_call" | custom-call | tf_op jit(solution)/shard_map/pallas_call | solution.py:696
  142.8 6.9 %shard_map.315 = (bf16[512,1024]{1,0:T(8,128)(2,1)}, f32[512,1024]{1,0:T(8,128)}, f32[1024,256]{1,0:T(8,128)}, f32[1024,256]{1,0:T(8,128)}, f32[1024,256]{1,0:T(...) custom-call(bf16[12,1024,128]{2,1,0:T(8,128)(2,1)} %get-tuple-elemen, ...), custom_call_target="tpu_custom_call" | custom-call | tf_op jit(solution)/shard_map/pallas_call | solution.py:753
